TPU v7x, 32 devices: a 4x4x1 block of a 4x4x8 slice. The times are simulated.
32 devices in a mesh: data: 1 (over z), wg: 32 (over y, x, core).
Axes of the slice: x: 4, y: 4, z: 1, core: 2. Of those that a mesh axis runs over, the one named last changes fastest.
The devices are a block of a 4x4x8 slice.
Arguments:
- hidden: bfloat16 [32, 512, 1600], P(('data', 'wg'))
- k_cache: bfloat16 [3, 32, 256, 25, 64], P(None, ('data', 'wg'))
- v_cache: bfloat16 [3, 32, 256, 25, 64], P(None, ('data', 'wg'))
- attn_gain: float32 [3, 1600], replicated
- attn_shift: float32 [3, 1600], replicated
- qkv_weight: bfloat16 [3, 1600, 3, 25, 64], P(None, 'wg')
- qkv_bias: float32 [3, 3, 25, 64], replicated
- out_weight: bfloat16 [3, 25, 64, 1600], P(None, None, None, 'wg')
- out_bias: float32 [3, 1600], replicated
- mlp_gain: float32 [3, 1600], replicated
- mlp_shift: float32 [3, 1600], replicated
- up_weight: bfloat16 [3, 1600, 6400], P(None, 'wg')
- up_bias: float32 [3, 6400], replicated
- down_weight: bfloat16 [3, 6400, 1600], P(None, None, 'wg')
- down_bias: float32 [3, 1600], replicated
- final_gain: float32 [1600], replicated
- final_shift: float32 [1600], replicated
Outputs:
- output 1: bfloat16 [32, 512, 1600], P(('data', 'wg'))
- output 2: bfloat16 [3, 32, 512, 25, 64], P(None, ('data', 'wg'))
- output 3: bfloat16 [3, 32, 512, 25, 64], P(None, ('data', 'wg'))
All inputs are finite; a program needn't handle non-finite values.
Results may differ from a plain program's by a relative error of at most 0.0141109.
Values are sent between devices in bfloat16 or wider.
A program may use at most 768 MiB of HBM per device.

v0:
```python
import jax
import jax.numpy as jnp
from jax import lax
from jax.sharding import PartitionSpec as P


def layer_norm(values, gain, shift):
    widened = values.astype(jnp.float32)
    mean_val = jnp.mean(widened, axis=-1, keepdims=True)
    centered = widened - mean_val
    variance = jnp.mean(centered * centered, axis=-1, keepdims=True)
    return centered * lax.rsqrt(variance + 1e-5) * gain + shift


def attention(query, cache_k, cache_v, key_new, value_new):
    new_len = query.shape[1]
    factor = query.shape[-1] ** -0.5
    prefix_scores = jnp.einsum("bthk,bshk->bhts", query, cache_k, preferred_element_type=jnp.float32) * factor
    self_scores = jnp.einsum("bthk,bshk->bhts", query, key_new, preferred_element_type=jnp.float32) * factor
    allowed = jnp.arange(new_len)[None, :] <= jnp.arange(new_len)[:, None]
    self_scores = jnp.where(allowed, self_scores, -1e30)
    row_max = jnp.maximum(jnp.max(prefix_scores, axis=-1, keepdims=True), jnp.max(self_scores, axis=-1, keepdims=True))
    prefix_exp = jnp.exp(prefix_scores - row_max)
    self_exp = jnp.exp(self_scores - row_max)
    denom_sum = jnp.sum(prefix_exp, axis=-1, keepdims=True) + jnp.sum(self_exp, axis=-1, keepdims=True)
    prefix_probs = (prefix_exp / denom_sum).astype(jnp.bfloat16)
    self_probs = (self_exp / denom_sum).astype(jnp.bfloat16)
    attended = jnp.einsum("bhts,bshk->bhtk", prefix_probs, cache_v, preferred_element_type=jnp.float32)
    attended = attended + jnp.einsum("bhts,bshk->bhtk", self_probs, value_new, preferred_element_type=jnp.float32)
    return attended.astype(jnp.bfloat16)


def decoder_layer(state, cache_k, cache_v, attn_gain, attn_shift, w_qkv, b_qkv, w_out, b_out, mlp_gain, mlp_shift, w_up, b_up, w_down, b_down):
    normed = layer_norm(state, attn_gain, attn_shift).astype(jnp.bfloat16)
    projected = (jnp.einsum("btd,dchk->btchk", normed, w_qkv, preferred_element_type=jnp.float32) + b_qkv).astype(jnp.bfloat16)
    query = projected[:, :, 0]
    key_new = projected[:, :, 1]
    value_new = projected[:, :, 2]
    attended = attention(query, cache_k, cache_v, key_new, value_new)
    attn_out = jnp.einsum("bhtk,hkd->btd", attended, w_out, preferred_element_type=jnp.float32) + b_out
    middle = (state.astype(jnp.float32) + attn_out).astype(jnp.bfloat16)
    normed_mlp = layer_norm(middle, mlp_gain, mlp_shift).astype(jnp.bfloat16)
    pre_act = jnp.einsum("btd,df->btf", normed_mlp, w_up, preferred_element_type=jnp.float32) + b_up
    activated = jax.nn.gelu(pre_act, approximate=True).astype(jnp.bfloat16)
    down_out = jnp.einsum("btf,fd->btd", activated, w_down, preferred_element_type=jnp.float32) + b_down
    new_state = (middle.astype(jnp.float32) + down_out).astype(jnp.bfloat16)
    return new_state, key_new, value_new


def solution(mesh):
    part_axis, group_axis = mesh.axis_names
    seq_spec = P((part_axis, group_axis))
    cache_spec = P(None, (part_axis, group_axis))
    replicated = P()
    in_specs = (seq_spec, cache_spec, cache_spec, replicated, replicated, P(None, group_axis), replicated,
                P(None, None, None, group_axis), replicated, replicated, replicated, P(None, group_axis), replicated,
                P(None, None, group_axis), replicated, replicated, replicated)
    out_specs = (seq_spec, cache_spec, cache_spec)

    def local_program(hidden, k_cache, v_cache, attn_gain, attn_shift, qkv_weight, qkv_bias, out_weight, out_bias, mlp_gain, mlp_shift, up_weight, up_bias, down_weight, down_bias, final_gain, final_shift):
        state = hidden
        keys_out = []
        values_out = []
        for layer_idx in range(qkv_weight.shape[0]):
            w_qkv = lax.all_gather(qkv_weight[layer_idx], group_axis, axis=0, tiled=True)
            w_out = lax.all_gather(out_weight[layer_idx], group_axis, axis=2, tiled=True)
            w_up = lax.all_gather(up_weight[layer_idx], group_axis, axis=0, tiled=True)
            w_down = lax.all_gather(down_weight[layer_idx], group_axis, axis=1, tiled=True)
            state, key_new, value_new = decoder_layer(
                state, k_cache[layer_idx], v_cache[layer_idx], attn_gain[layer_idx], attn_shift[layer_idx],
                w_qkv, qkv_bias[layer_idx], w_out, out_bias[layer_idx], mlp_gain[layer_idx], mlp_shift[layer_idx],
                w_up, up_bias[layer_idx], w_down, down_bias[layer_idx])
            keys_out.append(key_new)
            values_out.append(value_new)
        output = layer_norm(state, final_gain, final_shift).astype(jnp.bfloat16)
        return output, jnp.stack(keys_out), jnp.stack(values_out)

    return jax.shard_map(local_program, mesh=mesh, in_specs=in_specs, out_specs=out_specs, check_vma=False)
```

profile of v0, /device:TPU:97, one launch (start us, length us, event | category | flops | bytes accessed | tf_op | source)
XLA Modules:
  0.0 1382.7 jit_solution(14192706644137247244)
XLA Ops:
  43.2 29.8 %all-gather.27.cloned.1.call-done = bf16[1,25,64,1600]{2,1,0,3:T(8,128)(2,1)} async-done(((bf16[1,25,64,50]{2,1,0,3:T(8,128)(2,1)}), bf16[1,25,64,1600]{2,1,0,3:T(8,128)(2,1)}) %all-gather.27.cloned.1.call-update) | async-done | bytes 5120016 | tf_op jit(solution)/shard_map/all_gather | solution.py:66
  73.0 16.3 %copy.49 = bf16[1,25,64,1600]{3,2,1,0:T(8,128)(2,1)} copy(bf16[1,25,64,1600]{2,1,0,3:T(8,128)(2,1)} %all-gather.27.cloned.1.call-done) | data formatting | bytes 10240000 | tf_op jit(solution)/shard_map/all_gather | solution.py:66
  89.3 43.9 %all-gather.35.cloned.1.call-done = bf16[1,25,64,1600]{2,1,0,3:T(8,128)(2,1)} async-done(((bf16[1,25,64,50]{2,1,0,3:T(8,128)(2,1)}), bf16[1,25,64,1600]{2,1,0,3:T(8,128)(2,1)}) %all-gather.35.cloned.1.call-update) | async-done | bytes 5120016 | tf_op jit(solution)/shard_map/all_gather | solution.py:66
  133.2 16.1 %copy.57 = bf16[1,25,64,1600]{3,2,1,0:T(8,128)(2,1)} copy(bf16[1,25,64,1600]{2,1,0,3:T(8,128)(2,1)} %all-gather.35.cloned.1.call-done) | data formatting | bytes 10240000 | tf_op jit(solution)/shard_map/all_gather | solution.py:66
  149.3 44.1 %all-gather.43.cloned.1.call-done = bf16[1,25,64,1600]{2,1,0,3:T(8,128)(2,1)} async-done(((bf16[1,25,64,50]{2,1,0,3:T(8,128)(2,1)}), bf16[1,25,64,1600]{2,1,0,3:T(8,128)(2,1)}) %all-gather.43.cloned.1.call-update) | async-done | bytes 5120016 | tf_op jit(solution)/shard_map/all_gather | solution.py:66
  193.4 16.1 %copy.65 = bf16[1,25,64,1600]{3,2,1,0:T(8,128)(2,1)} copy(bf16[1,25,64,1600]{2,1,0,3:T(8,128)(2,1)} %all-gather.43.cloned.1.call-done) | data formatting | bytes 10240000 | tf_op jit(solution)/shard_map/all_gather | solution.py:66
  209.5 109.5 %all-gather.25.cloned.1.call-done = bf16[1,1600,3,25,64]{4,3,2,0,1:T(8,128)(2,1)} async-done(((bf16[1,50,3,25,64]{4,3,2,0,1:T(8,128)(2,1)}), bf16[1,1600,3,25,64]{4,3,2,0,1:T(8,128)(2,1)}) %all-gather.25.cloned.1.call-update) | async-done | bytes 15360016 | tf_op jit(solution)/shard_map/all_gather | solution.py:65
  318.9 45.9 %copy.45 = bf16[1,1600,3,25,64]{1,4,3,2,0:T(8,128)(2,1)} copy(bf16[1,1600,3,25,64]{4,3,2,0,1:T(8,128)(2,1)} %all-gather.25.cloned.1.call-done) | data formatting | bytes 30720000 | tf_op jit(solution)/shard_map/all_gather | solution.py:65
  396.1 16.6 %fusion.21 = f32[25,512]{1,0:T(8,128)S(1)} fusion(f32[25,512,512]{1,2,0:T(8,128)} %get-tuple-element.48, f32[25,512]{1,0:T(8,128)S(1)} %max.24, pred[512,512]{0,1:T(8,128)(4,1)S(1)} %iota_compare_fusion), kind=kLoop, calls=%fused_computation.30 | loop fusion | flops 26201600 | bytes 26578944 | tf_op jit(solution)/shard_map/reduce_sum | solution.py:25
  443.6 45.9 %copy.53 = bf16[1,1600,3,25,64]{1,4,3,2,0:T(8,128)(2,1)} copy(bf16[1,1600,3,25,64]{4,3,2,0,1:T(8,128)(2,1)} %all-gather.33.cloned.1.call-done) | data formatting | bytes 30720000 | tf_op jit(solution)/shard_map/all_gather | solution.py:65
  489.5 78.8 %all-gather.41.cloned.1.call-done = bf16[1,1600,3,25,64]{4,3,2,0,1:T(8,128)(2,1)} async-done(((bf16[1,50,3,25,64]{4,3,2,0,1:T(8,128)(2,1)}), bf16[1,1600,3,25,64]{4,3,2,0,1:T(8,128)(2,1)}) %all-gather.41.cloned.1.call-update) | async-done | bytes 15360016 | tf_op jit(solution)/shard_map/all_gather | solution.py:65
  568.3 45.9 %copy.61 = bf16[1,1600,3,25,64]{1,4,3,2,0:T(8,128)(2,1)} copy(bf16[1,1600,3,25,64]{4,3,2,0,1:T(8,128)(2,1)} %all-gather.41.cloned.1.call-done) | data formatting | bytes 30720000 | tf_op jit(solution)/shard_map/all_gather | solution.py:65
  614.2 83.3 %all-gather.29.cloned.1.call-done = bf16[1,1600,6400]{2,0,1:T(2,128)(2,1)} async-done(((bf16[1,50,6400]{2,0,1:T(2,128)(2,1)}), bf16[1,1600,6400]{2,0,1:T(2,128)(2,1)}) %all-gather.29.cloned.1.call-update) | async-done | bytes 20480016 | tf_op jit(solution)/shard_map/all_gather | solution.py:67
  697.5 26.0 %fusion.31.clone.3.clone.2 = bf16[512,6400]{1,0:T(8,128)(2,1)} fusion(bf16[1,1600,6400]{2,0,1:T(2,128)(2,1)} %all-gather.29.cloned.1.call-done, f32[6400]{0:T(1024)S(1)} %copy-done.20, bf16[1,512,1600]{1,2,0:T(8,128)(2,1)S(1)} %copy-done.11, f32[1600]{0:T(1024)S(1)} %copy-done.43, f32[1600]{0:T(1024)S(1)} %copy-done.33, ...), kind=kOutput, calls=%fused_computation.43.clone.clone.clone.clone.clone.clone.clone | convolution fusion | flops 10523443200 | bytes 28714496 | tf_op jit(solution)/shard_map/btd,df->btf/dot_general | solution.py:43
  723.5 103.1 %all-gather.31.cloned.1.call-done = bf16[1,6400,1600]{1,0,2:T(2,128)(2,1)} async-done(((bf16[1,6400,50]{1,0,2:T(2,128)(2,1)}), bf16[1,6400,1600]{1,0,2:T(2,128)(2,1)}) %all-gather.31.cloned.1.call-update) | async-done | bytes 20480016 | tf_op jit(solution)/shard_map/all_gather | solution.py:68
  826.6 20.6 %convert_reduce_fusion.3 = (f32[512]{0:T(512)S(1)}, bf16[1,512,1600]{1,2,0:T(8,128)(2,1)}) fusion(f32[1600]{0:T(1024)S(1)} %copy-done.42, bf16[1,6400,1600]{1,0,2:T(2,128)(2,1)} %all-gather.31.cloned.1.call-done, bf16[1,512,1600]{1,2,0:T(8,128)(2,1)S(1)} %copy-done.11, bf16[512,6400]{1,0:T(8,128)(2,1)} %fusion.31.clone.3.clone.2), kind=kOutput, calls=%fused_computation.118 | convolution fusion | flops 10490675200 | bytes 30318848 | tf_op jit(solution)/shard_map/btf,fd->btd/dot_general | solution.py:45
  926.1 29.6 %all-gather.37.cloned.1.call-done = bf16[1,1600,6400]{2,0,1:T(2,128)(2,1)} async-done(((bf16[1,50,6400]{2,0,1:T(2,128)(2,1)}), bf16[1,1600,6400]{2,0,1:T(2,128)(2,1)}) %all-gather.37.cloned.1.call-update) | async-done | bytes 20480016 | tf_op jit(solution)/shard_map/all_gather | solution.py:67
  955.8 25.9 %fusion.39.clone.3.clone.4 = bf16[512,6400]{1,0:T(8,128)(2,1)} fusion(bf16[1,1600,6400]{2,0,1:T(2,128)(2,1)} %all-gather.37.cloned.1.call-done, f32[6400]{0:T(1024)S(1)} %copy-done.19, bf16[1,512,1600]{1,2,0:T(8,128)(2,1)} %get-tuple-element.58, f32[1600]{0:T(1024)S(1)} %copy-done.39, f32[1600]{0:T(1024)S(1)} %copy-done.31, ...), kind=kOutput, calls=%fused_computation.51.clone.clone.clone.clone.clone.clone.clone.1 | convolution fusion | flops 10523443200 | bytes 28714496 | tf_op jit(solution)/shard_map/btd,df->btf/dot_general | solution.py:43
  981.7 103.1 %all-gather.39.cloned.1.call-done = bf16[1,6400,1600]{1,0,2:T(2,128)(2,1)} async-done(((bf16[1,6400,50]{1,0,2:T(2,128)(2,1)}), bf16[1,6400,1600]{1,0,2:T(2,128)(2,1)}) %all-gather.39.cloned.1.call-update) | async-done | bytes 20480016 | tf_op jit(solution)/shard_map/all_gather | solution.py:68
  1084.8 19.7 %convert_reduce_fusion.1 = (f32[512]{0:T(512)S(1)}, bf16[1,512,1600]{1,2,0:T(8,128)(2,1)S(1)}) fusion(f32[1600]{0:T(1024)S(1)} %copy-done.38, bf16[1,6400,1600]{1,0,2:T(2,128)(2,1)} %all-gather.39.cloned.1.call-done, bf16[1,512,1600]{1,2,0:T(8,128)(2,1)} %get-tuple-element.58, bf16[512,6400]{1,0:T(8,128)(2,1)} %fusion.39.clone.3.clone.4), kind=kOutput, calls=%fused_computation.112 | convolution fusion | flops 10490675200 | bytes 30318848 | tf_op jit(solution)/shard_map/btf,fd->btd/dot_general | solution.py:45
  1189.2 24.8 %all-gather.45.cloned.1.call-done = bf16[1,1600,6400]{2,0,1:T(2,128)(2,1)} async-done(((bf16[1,50,6400]{2,0,1:T(2,128)(2,1)}), bf16[1,1600,6400]{2,0,1:T(2,128)(2,1)}) %all-gather.45.cloned.1.call-update) | async-done | bytes 20480016 | tf_op jit(solution)/shard_map/all_gather | solution.py:67
  1214.0 25.4 %fusion.47.clone.3.clone.2 = bf16[512,6400]{1,0:T(8,128)(2,1)} fusion(bf16[1,1600,6400]{2,0,1:T(2,128)(2,1)} %all-gather.45.cloned.1.call-done, f32[6400]{0:T(1024)S(1)} %copy-done.18, bf16[1,512,1600]{1,2,0:T(8,128)(2,1)S(1)} %copy-done.12, f32[1600]{0:T(1024)S(1)} %copy-done.35, f32[1600]{0:T(1024)S(1)} %copy-done.29, ...), kind=kOutput, calls=%fused_computation.59.clone.clone.clone.clone.clone.clone.clone | convolution fusion | flops 10523443200 | bytes 28714496 | tf_op jit(solution)/shard_map/btd,df->btf/dot_general | solution.py:43
  1239.4 103.6 %all-gather.47.cloned.1.call-done = bf16[1,6400,1600]{1,0,2:T(2,128)(2,1)} async-done(((bf16[1,6400,50]{1,0,2:T(2,128)(2,1)}), bf16[1,6400,1600]{1,0,2:T(2,128)(2,1)}) %all-gather.47.cloned.1.call-update) | async-done | bytes 20480016 | tf_op jit(solution)/shard_map/all_gather | solution.py:68
  1342.9 21.0 %convert_reduce_fusion.6 = (f32[512]{0:T(512)S(1)}, bf16[1,512,1600]{1,2,0:T(8,128)(2,1)}) fusion(f32[1600]{0:T(1024)S(1)} %copy-done.34, bf16[1,6400,1600]{1,0,2:T(2,128)(2,1)} %all-gather.47.cloned.1.call-done, bf16[1,512,1600]{1,2,0:T(8,128)(2,1)} %get-tuple-element.66, bf16[512,6400]{1,0:T(8,128)(2,1)} %fusion.47.clone.3.clone.2), kind=kOutput, calls=%fused_computation.126 | convolution fusion | flops 10490675200 | bytes 30318848 | tf_op jit(solution)/shard_map/btf,fd->btd/dot_general | solution.py:45
  (193 shorter events, 272.6 us)
Async XLA Ops:
  7.2 65.8 %all-gather.27.cloned.1.call-start = ((), (), s32[]{:S(2)}) async-start(), calls=%async_computation.1 | async-start | bytes 13516800 | tf_op jit(solution)/shard_map/all_gather | solution.py:66
  9.4 123.8 %all-gather.35.cloned.1.call-start = ((), (), s32[]{:S(2)}) async-start(), calls=%async_computation.5 | async-start | bytes 13516800 | tf_op jit(solution)/shard_map/all_gather | solution.py:66
  10.4 183.0 %all-gather.43.cloned.1.call-start = ((), (), s32[]{:S(2)}) async-start(), calls=%async_computation.9 | async-start | bytes 13516800 | tf_op jit(solution)/shard_map/all_gather | solution.py:66
  11.3 307.6 %all-gather.25.cloned.1.call-start = ((), (), s32[]{:S(2)}) async-start(), calls=%async_computation | async-start | bytes 40550400 | tf_op jit(solution)/shard_map/all_gather | solution.py:65
  15.2 428.5 %all-gather.33.cloned.1.call-start = ((), (), s32[]{:S(2)}) async-start(), calls=%async_computation.4 | async-start | bytes 40550400 | tf_op jit(solution)/shard_map/all_gather | solution.py:65
  16.6 551.8 %all-gather.41.cloned.1.call-start = ((), (), s32[]{:S(2)}) async-start(), calls=%async_computation.8 | async-start | bytes 40550400 | tf_op jit(solution)/shard_map/all_gather | solution.py:65
  17.9 679.5 %all-gather.29.cloned.1.call-start = ((), (), s32[]{:S(2)}) async-start(), calls=%async_computation.2 | async-start | bytes 42240000 | tf_op jit(solution)/shard_map/all_gather | solution.py:67
  21.9 804.8 %all-gather.31.cloned.1.call-start = ((), (), s32[]{:S(2)}) async-start(), calls=%async_computation.3 | async-start | bytes 42240000 | tf_op jit(solution)/shard_map/all_gather | solution.py:68
  26.8 929.0 %all-gather.37.cloned.1.call-start = ((), (), s32[]{:S(2)}) async-start(), calls=%async_computation.6 | async-start | bytes 42240000 | tf_op jit(solution)/shard_map/all_gather | solution.py:67
  29.0 1055.8 %all-gather.39.cloned.1.call-start = ((), (), s32[]{:S(2)}) async-start(), calls=%async_computation.7 | async-start | bytes 42240000 | tf_op jit(solution)/shard_map/all_gather | solution.py:68
  32.5 1181.4 %all-gather.45.cloned.1.call-start = ((), (), s32[]{:S(2)}) async-start(), calls=%async_computation.10 | async-start | bytes 42240000 | tf_op jit(solution)/shard_map/all_gather | solution.py:67
  34.8 1308.1 %all-gather.47.cloned.1.call-start = ((), (), s32[]{:S(2)}) async-start(), calls=%async_computation.11 | async-start | bytes 42240000 | tf_op jit(solution)/shard_map/all_gather | solution.py:68
  489.5 208.0 %copy-start.11 = (bf16[1,512,1600]{1,2,0:T(8,128)(2,1)S(1)}, bf16[1,512,1600]{1,2,0:T(8,128)(2,1)}, u32[]{:S(2)}) copy-start(bf16[1,512,1600]{1,2,0:T(8,128)(2,1)} %get-tuple-element.50) | copy-start | bytes 4915204
  489.5 208.0 %copy-start.20 = (f32[6400]{0:T(1024)S(1)}, f32[6400]{0:T(1024)}, u32[]{:S(2)}) copy-start(f32[6400]{0:T(1024)} %get-tuple-element.4) | copy-start | bytes 76804
  489.5 208.0 %copy-start.33 = (f32[1600]{0:T(1024)S(1)}, f32[1600]{0:T(1024)}, u32[]{:S(2)}) copy-start(f32[1600]{0:T(1024)} %get-tuple-element.7) | copy-start | bytes 19204
  489.5 208.0 %copy-start.43 = (f32[1600]{0:T(1024)S(1)}, f32[1600]{0:T(1024)}, u32[]{:S(2)}) copy-start(f32[1600]{0:T(1024)} %get-tuple-element.73) | copy-start | bytes 19204
  697.5 129.1 %copy-start.42 = (f32[1600]{0:T(1024)S(1)}, f32[1600]{0:T(1024)}, u32[]{:S(2)}) copy-start(f32[1600]{0:T(1024)} %get-tuple-element.13) | copy-start | bytes 19204
  911.4 44.4 %copy-start.19 = (f32[6400]{0:T(1024)S(1)}, f32[6400]{0:T(1024)}, u32[]{:S(2)}) copy-start(f32[6400]{0:T(1024)} %get-tuple-element.5) | copy-start | bytes 76804
  911.4 44.4 %copy-start.31 = (f32[1600]{0:T(1024)S(1)}, f32[1600]{0:T(1024)}, u32[]{:S(2)}) copy-start(f32[1600]{0:T(1024)} %get-tuple-element.8) | copy-start | bytes 19204
  911.4 44.4 %copy-start.39 = (f32[1600]{0:T(1024)S(1)}, f32[1600]{0:T(1024)}, u32[]{:S(2)}) copy-start(f32[1600]{0:T(1024)} %get-tuple-element.72) | copy-start | bytes 19204
  955.8 129.0 %copy-start.38 = (f32[1600]{0:T(1024)S(1)}, f32[1600]{0:T(1024)}, u32[]{:S(2)}) copy-start(f32[1600]{0:T(1024)} %get-tuple-element.14) | copy-start | bytes 19204
  1185.0 28.9 %copy-start.29 = (f32[1600]{0:T(1024)S(1)}, f32[1600]{0:T(1024)}, u32[]{:S(2)}) copy-start(f32[1600]{0:T(1024)} %get-tuple-element.6) | copy-start | bytes 19204
  1185.0 28.9 %copy-start.35 = (f32[1600]{0:T(1024)S(1)}, f32[1600]{0:T(1024)}, u32[]{:S(2)}) copy-start(f32[1600]{0:T(1024)} %get-tuple-element.74) | copy-start | bytes 19204
  1213.9 129.0 %copy-start.34 = (f32[1600]{0:T(1024)S(1)}, f32[1600]{0:T(1024)}, u32[]{:S(2)}) copy-start(f32[1600]{0:T(1024)} %get-tuple-element.12) | copy-start | bytes 19204
  (32 other events, 382.4 us)
Sparse Core Ops, SparseCore 0:
  10.1 62.8 all-gather.26
  75.1 58.0 all-gather.34
  135.3 58.0 all-gather.42
  195.9 123.0 all-gather.24
  320.9 122.7 all-gather.32
  445.6 122.7 all-gather.40
  570.5 126.9 all-gather.28
  699.6 126.9 all-gather.30
  828.8 126.9 all-gather.36
  957.8 126.9 all-gather.38
  1086.9 126.9 all-gather.44
  1215.9 126.9 all-gather.46
where the time goes:
time: 1400 us; the launch traced here: 1380 us
  waiting for transfers between devices  754 us (54%)
  matrix products  307 us (22%)
  local copies, waits for them, and re-layouts  235 us (17%)
  other arithmetic  70.8 us (5%)
  between operations  15.2 us (1%)
    all_gather x3, waiting for transfers between devices, local_program(): lax.all_gather(down_weight[layer_idx], group_axis, axis=1, tiled=True)  310 us
    all_gather x3, waiting for transfers between devices, local_program(): lax.all_gather(qkv_weight[layer_idx], group_axis, axis=0, tiled=True)  188 us
    all_gather x3, waiting for transfers between devices, local_program(): w_up = lax.all_gather(up_weight[layer_idx], group_axis, axis=0, tiled=True)  138 us
    all_gather x3, local copies, waits for them, and re-layouts, local_program(): lax.all_gather(qkv_weight[layer_idx], group_axis, axis=0, tiled=True)  138 us
    all_gather x3, waiting for transfers between devices, local_program(): lax.all_gather(out_weight[layer_idx], group_axis, axis=2, tiled=True)  118 us
    dot_general x3, matrix products, decoder_layer(): jnp.einsum('btd,df->btf', normed_mlp, w_up, preferred_element_type=jnp.fl...  77.3 us
    dot_general x3, matrix products, decoder_layer(): jnp.einsum('btf,fd->btd', activated, w_down, preferred_element_type=jnp.f...  61.3 us
    all_gather x3, local copies, waits for them, and re-layouts, local_program(): lax.all_gather(out_weight[layer_idx], group_axis, axis=2, tiled=True)  48.5 us
  transfers between devices with their start and end apart: 12, of which 12 were waited for; matrix products, arithmetic and copies ran while one was open for 41% of the time, Pallas kernels for 0%

commit v1 on v0

--- a/solution.py
+++ b/solution.py
@@ -1,7 +1,202 @@
+import functools
+import math
+
 import jax
 import jax.numpy as jnp
 from jax import lax
+from jax.experimental import pallas as pl
+from jax.experimental.pallas import tpu as pltpu
 from jax.sharding import PartitionSpec as P
+
+MESH = pl.DeviceIdType.MESH
+LANES = 128
+
+
+class Torus:
+    def __init__(self, axis, side, send_sem, recv_sem, local_sem):
+        me = lax.axis_index(axis)
+        self.axis, self.side = axis, side
+        self.core = lax.rem(me, 2)
+        self.x = lax.rem(me // 2, side)
+        self.y = me // (2 * side)
+        self.send_sem, self.recv_sem, self.local_sem = send_sem, recv_sem, local_sem
+
+    def coord(self, dim, k):
+        return lax.rem((self.x if dim == "x" else self.y) + (k + self.side), self.side)
+
+    def device(self, y, x, core):
+        return {self.axis: (y * self.side + x) * 2 + core}
+
+    def step(self, dim, k):
+        if dim == "x":
+            return self.device(self.y, self.coord("x", k), self.core)
+        return self.device(self.coord("y", k), self.x, self.core)
+
+    def partner(self):
+        return self.device(self.y, self.x, 1 - self.core)
+
+    def meet(self):
+        barrier = pltpu.get_barrier_semaphore()
+        peers = [self.step(dim, k) for dim in ("x", "y") for k in (1, -1)] + [self.partner()]
+        for peer in peers:
+            pl.semaphore_signal(barrier, inc=1, device_id=peer, device_id_type=MESH)
+        pl.semaphore_wait(barrier, len(peers))
+
+
+class Unit:
+    def __init__(self, torus, index, shard, landing):
+        self.torus, self.index, self.shard, self.landing = torus, index, shard, landing
+        half = shard.shape[-1] // LANES // 2 * LANES
+        self.columns = (pl.ds(0, half), pl.ds(half, shard.shape[-1] - half))
+        self.rank = len(shard.shape)
+        cut = shard.shape[0] // 2
+        self.rows = (slice(None), pl.ds(0, cut), pl.ds(cut, shard.shape[0] - cut))
+
+    def _tail(self, t, part):
+        return (self.rows[part],) + (slice(None),) * (self.rank - 2) + (self.columns[t],)
+
+    def own(self, t):
+        return self.shard.at[self._tail(t, 0)]
+
+    def piece(self, t, k, part=0):
+        torus = self.torus
+        where = (torus.y, torus.coord("x", k)) if t == 0 else (torus.coord("y", k), torus.x)
+        return self.landing.at[(torus.core,) + where + self._tail(t, part)]
+
+    def block(self, t, k, part=0):
+        torus = self.torus
+        where = (torus.coord("y", k), slice(None)) if t == 0 else (slice(None), torus.coord("x", k))
+        return self.landing.at[(torus.core,) + where + self._tail(t, part)]
+
+    def copy(self, t, slot):
+        torus = self.torus
+        first, second = ("x", "y") if t == 0 else ("y", "x")
+        source, target, device = {
+            0: lambda: (self.own(t), self.piece(t, 0), torus.step(first, 1)),
+            1: lambda: (self.own(t), self.piece(t, 0), torus.step(first, -1)),
+            2: lambda: (self.piece(t, -1, 1), None, torus.step(first, 1)),
+            3: lambda: (self.piece(t, 1, 2), None, torus.step(first, -1)),
+            4: lambda: (self.block(t, 0), None, torus.step(second, 1)),
+            5: lambda: (self.block(t, 0), None, torus.step(second, -1)),
+            6: lambda: (self.block(t, -1, 1), None, torus.step(second, 1)),
+            7: lambda: (self.block(t, 1, 2), None, torus.step(second, -1)),
+            8: lambda: (self.block(t, 0), None, torus.partner()),
+            9: lambda: (self.block(t, -1), None, torus.partner()),
+            10: lambda: (self.block(t, 1), None, torus.partner()),
+            11: lambda: (self.block(t, 2), None, torus.partner()),
+        }[slot]()
+        return pltpu.make_async_remote_copy(
+            src_ref=source, dst_ref=source if target is None else target,
+            send_sem=torus.send_sem.at[self.index, t, slot], recv_sem=torus.recv_sem.at[self.index, t, slot],
+            device_id=device, device_id_type=MESH)
+
+    def keep(self, t):
+        return pltpu.make_async_copy(self.own(t), self.piece(t, 0), self.torus.local_sem.at[self.index, t])
+
+    def start(self, *slots):
+        for t in range(2):
+            for slot in slots:
+                self.copy(t, slot).start()
+
+    def arrived(self, *slots):
+        for t in range(2):
+            for slot in slots:
+                self.copy(t, slot).wait_recv()
+
+    def send_own(self):
+        self.start(0, 1)
+        for t in range(2):
+            self.keep(t).start()
+
+    def relay_own(self):
+        self.arrived(0, 1)
+        self.start(2, 3)
+
+    def send_block(self):
+        for t in range(2):
+            self.keep(t).wait()
+        self.arrived(2, 3)
+        self.start(4, 5, 8)
+
+    def relay_block(self):
+        self.arrived(4, 5)
+        self.start(6, 7, 9, 10)
+
+    def last_block(self):
+        self.arrived(6, 7)
+        self.start(11)
+
+    def complete(self):
+        self.arrived(8, 9, 10, 11)
+
+    def drain(self):
+        for t in range(2):
+            for slot in range(12):
+                self.copy(t, slot).wait_send()
+
+
+def gather_kernel(axis, side, shard, extra, landing, landing_extra, send_sem, recv_sem, local_sem):
+    torus = Torus(axis, side, send_sem, recv_sem, local_sem)
+    torus.meet()
+    count = shard.shape[0]
+    rest = Unit(torus, count, extra, landing_extra)
+
+    def unit(u):
+        return Unit(torus, u, shard.at[u], landing.at[u])
+
+    rest.send_own()
+    rest.relay_own()
+    unit(0).send_own()
+    rest.send_block()
+    unit(0).relay_own()
+    rest.relay_block()
+
+    def turn(u, carry):
+        @pl.when(u + 1 < count)
+        def _():
+            unit(u + 1).send_own()
+
+        unit(u).send_block()
+
+        @pl.when(u + 1 < count)
+        def _():
+            unit(u + 1).relay_own()
+
+        @pl.when(u > 0)
+        def _():
+            unit(u - 1).last_block()
+            unit(u - 1).complete()
+
+        unit(u).relay_block()
+        return carry
+
+    lax.fori_loop(0, count, turn, 0)
+    rest.last_block()
+    rest.complete()
+    unit(count - 1).last_block()
+    unit(count - 1).complete()
+    rest.drain()
+
+    def drain(u, carry):
+        unit(u).drain()
+        return carry
+
+    lax.fori_loop(0, count, drain, 0)
+
+
+def gather_all(axis, size, shard, extra):
+    side = math.isqrt(size // 2)
+    count, rows, columns = shard.shape
+    return pl.pallas_call(
+        functools.partial(gather_kernel, axis, side),
+        out_shape=(jax.ShapeDtypeStruct((count, 2, side, side, rows, columns), shard.dtype),
+                   jax.ShapeDtypeStruct((2, side, side) + extra.shape, extra.dtype)),
+        in_specs=[pl.BlockSpec(memory_space=pltpu.VMEM)] * 2,
+        out_specs=(pl.BlockSpec(memory_space=pl.ANY),) * 2,
+        scratch_shapes=[pltpu.SemaphoreType.DMA((count + 1, 2, 12)), pltpu.SemaphoreType.DMA((count + 1, 2, 12)),
+                        pltpu.SemaphoreType.DMA((count + 1, 2))],
+        compiler_params=pltpu.CompilerParams(collective_id=0, has_side_effects=True, vmem_limit_bytes=32 * 2**20),
+    )(shard, extra)
 
 
 def layer_norm(values, gain, shift):
@@ -59,13 +254,32 @@
 
     def local_program(hidden, k_cache, v_cache, attn_gain, attn_shift, qkv_weight, qkv_bias, out_weight, out_bias, mlp_gain, mlp_shift, up_weight, up_bias, down_weight, down_bias, final_gain, final_shift):
         state = hidden
+        layers, depth = up_weight.shape[0], up_weight.shape[1]
+        inner = out_weight.shape[1] * out_weight.shape[2]
+        wide = up_weight.shape[2]
+        heads, head_dim = out_weight.shape[1:3]
+        model = hidden.shape[-1]
+        even = depth // 16 * 16
+        w_q = qkv_weight.reshape(layers, depth, 3 * inner)
+        w_o = jnp.transpose(out_weight, (0, 3, 1, 2)).reshape(layers, depth, inner)
+        w_d = jnp.swapaxes(down_weight, 1, 2)
+        shards = jnp.stack([jnp.concatenate([w_q, w_o], axis=2), up_weight, w_d], axis=1)
+        shards = shards.reshape(layers * 3, depth, wide)
+        main, rest = gather_all(group_axis, mesh.shape[group_axis], shards[:, :even], shards[:, even:])
+
+        def whole(unit):
+            a = jnp.transpose(main[unit], (1, 2, 0, 3, 4))
+            b = jnp.transpose(rest[:, :, :, unit], (1, 2, 0, 3, 4))
+            return jnp.concatenate([a, b], axis=3).reshape(model, wide)
+
         keys_out = []
         values_out = []
         for layer_idx in range(qkv_weight.shape[0]):
-            w_qkv = lax.all_gather(qkv_weight[layer_idx], group_axis, axis=0, tiled=True)
-            w_out = lax.all_gather(out_weight[layer_idx], group_axis, axis=2, tiled=True)
-            w_up = lax.all_gather(up_weight[layer_idx], group_axis, axis=0, tiled=True)
-            w_down = lax.all_gather(down_weight[layer_idx], group_axis, axis=1, tiled=True)
+            mixed = whole(3 * layer_idx)
+            w_qkv = mixed[:, :3 * inner].reshape(model, 3, heads, head_dim)
+            w_out = jnp.transpose(mixed[:, 3 * inner:]).reshape(heads, head_dim, model)
+            w_up = whole(3 * layer_idx + 1)
+            w_down = jnp.transpose(whole(3 * layer_idx + 2))
             state, key_new, value_new = decoder_layer(
                 state, k_cache[layer_idx], v_cache[layer_idx], attn_gain[layer_idx], attn_shift[layer_idx],
                 w_qkv, qkv_bias[layer_idx], w_out, out_bias[layer_idx], mlp_gain[layer_idx], mlp_shift[layer_idx],

time: 1400 us -> 1490 us (1.064)
  waiting for transfers between devices: 754 us -> 0 us
  Pallas kernels: 0 us -> 485 us
  local copies, waits for them, and re-layouts: 235 us -> 492 us
  other arithmetic: 70.8 us -> 208 us
  matrix products: 307 us -> 285 us
    all_gather x12 -> x0, waiting for transfers between devices: 754 us -> none  [the longest x3 310 us: local_program(): lax.all_gather(down_weight[layer_idx], group_axis, axis=1, tiled=True)]
    pallas_call x0 -> x1, Pallas kernels: none -> 485 us  [gather_all(): pl.pallas_call(functools.partial(gather_kernel, axis, side), out_shape=(j...]
    all_gather x6 -> x0, local copies, waits for them, and re-layouts: 186 us -> none  [the longest x3 138 us: local_program(): lax.all_gather(qkv_weight[layer_idx], group_axis, axis=0, tiled=True)]
    transpose x0 -> x9, local copies, waits for them, and re-layouts: none -> 175 us  [the longest x1 113 us: whole(): a = jnp.transpose(main[unit], (1, 2, 0, 3, 4))]
    reshape x0 -> x11, local copies, waits for them, and re-layouts: none -> 171 us  [the longest x9 165 us: whole(): return jnp.concatenate([a, b], axis=3).reshape(model, wide)]
    concatenate x0 -> x9, local copies, waits for them, and re-layouts: none -> 133 us  [whole(): return jnp.concatenate([a, b], axis=3).reshape(model, wide)]
    concatenate x0 -> x5, other arithmetic: none -> 125 us  [whole(): return jnp.concatenate([a, b], axis=3).reshape(model, wide)]
    unnamed x100 -> x103, local copies, waits for them, and re-layouts: 26.6 us -> 7.58 us
  transfers between devices with their start and end apart: 12 -> 0, of which waited for: 12 -> 0; matrix products, arithmetic and copies ran while one was open for 41% -> 0% of each run, Pallas kernels for 0% -> 0%
where the time goes in v1:
time: 1490 us; the launch traced here: 1470 us
  local copies, waits for them, and re-layouts  492 us (33%)
  Pallas kernels  485 us (33%)
  matrix products  285 us (19%)
  other arithmetic  208 us (14%)
    pallas_call x1, Pallas kernels, gather_all(): pl.pallas_call(functools.partial(gather_kernel, axis, side), out_shape=(j...  485 us
    reshape x9, local copies, waits for them, and re-layouts, whole(): return jnp.concatenate([a, b], axis=3).reshape(model, wide)  165 us
    concatenate x9, local copies, waits for them, and re-layouts, whole(): return jnp.concatenate([a, b], axis=3).reshape(model, wide)  133 us
    concatenate x5, other arithmetic, whole(): return jnp.concatenate([a, b], axis=3).reshape(model, wide)  125 us
    transpose x1, local copies, waits for them, and re-layouts, whole(): a = jnp.transpose(main[unit], (1, 2, 0, 3, 4))  113 us
    dot_general x3, matrix products, decoder_layer(): jnp.einsum('btd,df->btf', normed_mlp, w_up, preferred_element_type=jnp.fl...  67.4 us
    dot_general x3, matrix products, decoder_layer(): jnp.einsum('btf,fd->btd', activated, w_down, preferred_element_type=jnp.f...  52 us
    transpose x6, local copies, waits for them, and re-layouts, local_program(): w_out = jnp.transpose(mixed[:, 3 * inner:]).reshape(heads, head_dim, model)  51.8 us

profile of v1, /device:TPU:97, one launch (start us, length us, event | category | flops | bytes accessed | tf_op | source)
XLA Modules:
  0.0 1472.2 jit_solution(11862777644781279359)
XLA Ops:
  16.3 484.9 %shard_map.184 = (bf16[9,2,4,4,48,6400]{5,4,3,2,1,0:T(8,128)(2,1)}, bf16[2,4,4,9,2,6400]{5,4,3,2,1,0:T(2,128)(2,1)S(1)}) custom-call(bf16[9,48,6400]{2,1,0:T(8,128)(2,1)S(1)} %slice.260.shard, bf16[9,2,6400]{2,1,0:T(2,128)(2,1)S(1)} %slice.261.extra), custom_call_target="tpu_custom_call" | custom-call | tf_op jit(solution)/shard_map/pallas_call | solution.py:190
  504.2 112.9 %slice_bitcast_fusion.1 = (bf16[4,4,2,48,6400]{4,3,1,0,2:T(8,128)(2,1)}, bf16[4,4,2,48,6400]{4,3,1,0,2:T(8,128)(2,1)}, bf16[4,4,2,48,6400]{4,3,1,0,2:T(8,128)(2,...) fusion(bf16[9,2,4,4,48,6400]{5,4,3,2,1,0:T(8,128)(2,1)} %get-tu, ...), kind=kLoop, calls=%fused_computation.26 | loop fusion | bytes 353894400 | tf_op jit(solution)/shard_map/transpose | solution.py:271
  625.5 29.0 %pad_maximum_fusion = (bf16[4,4,2,50,6400]{4,3,1,0,2:T(8,128)(2,1)}, bf16[4,4,2,50,6400]{4,3,1,0,2:T(8,128)(2,1)}) fusion(bf16[4,4,2,2,6400]{4,3,1,0,2:T(2,128)(2,1)S(1)} %get-tuple-element.45, bf16[4,4,2,48,6400]{4,3,1,0,2:T(8,128)(2,1)} %get-tuple-element.36, bf16[4,4,2,2,6400]{4,3,1,0,2:T(2,128)(2,1)S(1)} %get-tuple-element.44, ...), kind=kLoop, calls=%fused_computation.12 | loop fusion | flops 81920000 | bytes 81920000 | tf_op jit(solution)/shard_map/concatenate | solution.py:273
  670.2 18.4 %reshape.608 = bf16[1600,6400]{1,0:T(8,128)(2,1)} reshape(bf16[4,4,2,50,6400]{4,3,2,1,0:T(8,128)(2,1)} %copy.26) | data formatting | bytes 40960000 | tf_op jit(solution)/shard_map/reshape | solution.py:273
  719.7 16.6 %fusion.3 = f32[25,512]{1,0:T(8,128)S(1)} fusion(f32[25,512,512]{1,2,0:T(8,128)} %get-tuple-element.58, f32[25,512]{1,0:T(8,128)S(1)} %max.24, pred[512,512]{0,1:T(8,128)(4,1)S(1)} %iota_compare_fusion), kind=kLoop, calls=%fused_computation.21 | loop fusion | flops 26201600 | bytes 26578944 | tf_op jit(solution)/shard_map/reduce_sum | solution.py:220
  800.6 18.4 %reshape.617 = bf16[1600,6400]{1,0:T(8,128)(2,1)} reshape(bf16[4,4,2,50,6400]{4,3,2,1,0:T(8,128)(2,1)} %copy.29) | data formatting | bytes 40960000 | tf_op jit(solution)/shard_map/reshape | solution.py:273
  821.2 22.8 %fusion.19.clone.1.clone.2 = bf16[512,6400]{1,0:T(8,128)(2,1)} fusion(bf16[1600,6400]{1,0:T(8,128)(2,1)} %reshape.617, f32[6400]{0:T(1024)S(1)} %get-tuple-element.8, bf16[1,512,1600]{1,2,0:T(8,128)(2,1)S(1)} %copy-done.18, f32[1600]{0:T(1024)S(1)} %get-tuple-element.91, f32[1600]{0:T(1024)S(1)} %get-tuple-element.11, ...), kind=kOutput, calls=%fused_computation.49.clone.clone.clone.clone.clone | convolution fusion | flops 10523443200 | bytes 28714496 | tf_op jit(solution)/shard_map/btd,df->btf/dot_general | solution.py:238
  844.0 29.0 %pad_maximum_fusion.2 = (bf16[4,4,2,50,6400]{4,3,1,0,2:T(8,128)(2,1)}, bf16[4,4,2,50,6400]{4,3,1,0,2:T(8,128)(2,1)}) fusion(bf16[4,4,2,2,6400]{4,3,1,0,2:T(2,128)(2,1)S(1)} %copy-done.17, bf16[4,4,2,48,6400]{4,3,1,0,2:T(8,128)(2,1)} %get-tuple-element.34, bf16[4,4,2,2,6400]{4,3,1,0,2:T(2,128)(2,1)S(1)} %copy-done.16, ...), kind=kLoop, calls=%fused_computation.14 | loop fusion | flops 81920000 | bytes 81920000 | tf_op jit(solution)/shard_map/concatenate | solution.py:273
  888.7 18.3 %reshape.618 = bf16[1600,6400]{1,0:T(8,128)(2,1)} reshape(bf16[4,4,2,50,6400]{4,3,2,1,0:T(8,128)(2,1)} %copy.30) | data formatting | bytes 40960000 | tf_op jit(solution)/shard_map/reshape | solution.py:273
  907.0 17.1 %convert_reduce_fusion.3 = (f32[512]{0:T(512)S(1)}, bf16[1,512,1600]{1,2,0:T(8,128)(2,1)S(1)}) fusion(f32[1600]{0:T(1024)S(1)} %get-tuple-element.17, bf16[1600,6400]{1,0:T(8,128)(2,1)} %reshape.618, bf16[1,512,1600]{1,2,0:T(8,128)(2,1)S(1)} %copy-done.18, bf16[512,6400]{1,0:T(8,128)(2,1)} %fusion.19.clone.1.clone.2), kind=kOutput, calls=%fused_computation.107 | convolution fusion | flops 10490675200 | bytes 30318848 | tf_op jit(solution)/shard_map/btf,fd->btd/dot_general | solution.py:240
  940.2 18.3 %reshape.620 = bf16[1600,6400]{1,0:T(8,128)(2,1)} reshape(bf16[4,4,2,50,6400]{4,3,2,1,0:T(8,128)(2,1)} %copy.31) | data formatting | bytes 40960000 | tf_op jit(solution)/shard_map/reshape | solution.py:273
  987.7 16.4 %fusion.4 = f32[25,512]{1,0:T(8,128)S(1)} fusion(f32[25,512,512]{1,2,0:T(8,128)} %get-tuple-element.66, f32[25,512]{1,0:T(8,128)S(1)} %max.25, pred[512,512]{0,1:T(8,128)(4,1)S(1)} %copy-done.8), kind=kLoop, calls=%fused_computation.22 | loop fusion | flops 26201600 | bytes 26578944 | tf_op jit(solution)/shard_map/reduce_sum | solution.py:220
  1052.6 28.4 %pad_maximum_fusion.4 = (bf16[4,4,2,50,6400]{4,3,1,0,2:T(8,128)(2,1)}, bf16[4,4,2,50,6400]{4,3,1,0,2:T(8,128)(2,1)}) fusion(bf16[4,4,2,2,6400]{4,3,1,0,2:T(2,128)(2,1)S(1)} %copy-done.15, bf16[4,4,2,48,6400]{4,3,1,0,2:T(8,128)(2,1)} %get-tuple-element.32, bf16[4,4,2,2,6400]{4,3,1,0,2:T(2,128)(2,1)S(1)} %copy-done.14, ...), kind=kLoop, calls=%fused_computation.16 | loop fusion | flops 81920000 | bytes 81920000 | tf_op jit(solution)/shard_map/concatenate | solution.py:273
  1096.7 18.4 %reshape.629 = bf16[1600,6400]{1,0:T(8,128)(2,1)} reshape(bf16[4,4,2,50,6400]{4,3,2,1,0:T(8,128)(2,1)} %copy.34) | data formatting | bytes 40960000 | tf_op jit(solution)/shard_map/reshape | solution.py:273
  1115.2 22.2 %fusion.27.clone.1.clone.4 = bf16[512,6400]{1,0:T(8,128)(2,1)} fusion(bf16[1600,6400]{1,0:T(8,128)(2,1)} %reshape.629, f32[6400]{0:T(1024)S(1)} %copy-done.26, bf16[1,512,1600]{1,2,0:T(8,128)(2,1)S(1)} %copy-done.20, f32[1600]{0:T(1024)S(1)} %copy-done.46, f32[1600]{0:T(1024)S(1)} %copy-done.38, f32[512]{0:T(512)S(1)} %add_rsqrt_fusion.3, ...), kind=kOutput, calls=%fused_computation.57.clone.clone.clone.clone.clone.1 | convolution fusion | flops 10523443200 | bytes 28714496 | tf_op jit(solution)/shard_map/btd,df->btf/dot_general | solution.py:238
  1153.0 18.3 %reshape.630 = bf16[1600,6400]{1,0:T(8,128)(2,1)} reshape(bf16[4,4,2,50,6400]{4,3,2,1,0:T(8,128)(2,1)} %copy.35) | data formatting | bytes 40960000 | tf_op jit(solution)/shard_map/reshape | solution.py:273
  1171.3 17.7 %convert_reduce_fusion.1 = (f32[512]{0:T(512)S(1)}, bf16[1,512,1600]{1,2,0:T(8,128)(2,1)S(1)}) fusion(f32[1600]{0:T(1024)S(1)} %copy-done.45, bf16[1600,6400]{1,0:T(8,128)(2,1)} %reshape.630, bf16[1,512,1600]{1,2,0:T(8,128)(2,1)} %get-tuple-element.68, bf16[512,6400]{1,0:T(8,128)(2,1)} %fusion.27.clone.1.clone.4), kind=kOutput, calls=%fused_computation.101 | convolution fusion | flops 10490675200 | bytes 30318848 | tf_op jit(solution)/shard_map/btf,fd->btd/dot_general | solution.py:240
  1189.5 29.0 %pad_maximum_fusion.6 = (bf16[4,4,2,50,6400]{4,3,1,0,2:T(8,128)(2,1)}, bf16[4,4,2,50,6400]{4,3,1,0,2:T(8,128)(2,1)}) fusion(bf16[4,4,2,2,6400]{4,3,1,0,2:T(2,128)(2,1)S(1)} %copy-done.13, bf16[4,4,2,48,6400]{4,3,1,0,2:T(8,128)(2,1)} %get-tuple-element.30, bf16[4,4,2,2,6400]{4,3,1,0,2:T(2,128)(2,1)S(1)} %copy-done.12, ...), kind=kLoop, calls=%fused_computation.18 | loop fusion | flops 81920000 | bytes 81920000 | tf_op jit(solution)/shard_map/concatenate | solution.py:273
  1234.1 18.4 %reshape.632 = bf16[1600,6400]{1,0:T(8,128)(2,1)} reshape(bf16[4,4,2,50,6400]{4,3,2,1,0:T(8,128)(2,1)} %copy.36) | data formatting | bytes 40960000 | tf_op jit(solution)/shard_map/reshape | solution.py:273
  1294.7 16.5 %fusion.5 = f32[25,512]{1,0:T(8,128)S(1)} fusion(f32[25,512,512]{1,2,0:T(8,128)} %get-tuple-element.74, f32[25,512]{1,0:T(8,128)S(1)} %max.26, pred[512,512]{0,1:T(8,128)(4,1)S(1)} %copy-done.9), kind=kLoop, calls=%fused_computation.23 | loop fusion | flops 26201600 | bytes 26578944 | tf_op jit(solution)/shard_map/reduce_sum | solution.py:220
  1375.1 18.4 %reshape.641 = bf16[1600,6400]{1,0:T(8,128)(2,1)} reshape(bf16[4,4,2,50,6400]{4,3,2,1,0:T(8,128)(2,1)} %copy.39) | data formatting | bytes 40960000 | tf_op jit(solution)/shard_map/reshape | solution.py:273
  1393.5 22.5 %fusion.35.clone.1.clone.2 = bf16[512,6400]{1,0:T(8,128)(2,1)} fusion(bf16[1600,6400]{1,0:T(8,128)(2,1)} %reshape.641, f32[6400]{0:T(1024)S(1)} %copy-done.25, bf16[1,512,1600]{1,2,0:T(8,128)(2,1)S(1)} %copy-done.19, f32[1600]{0:T(1024)S(1)} %copy-done.40, f32[1600]{0:T(1024)S(1)} %copy-done.36, f32[512]{0:T(512)S(1)} %add_rsqrt_fusion.1, ...), kind=kOutput, calls=%fused_computation.65.clone.clone.clone.clone.clone | convolution fusion | flops 10523443200 | bytes 28714496 | tf_op jit(solution)/shard_map/btd,df->btf/dot_general | solution.py:238
  1433.8 18.3 %reshape.642 = bf16[1600,6400]{1,0:T(8,128)(2,1)} reshape(bf16[4,4,2,50,6400]{4,3,2,1,0:T(8,128)(2,1)} %copy.40) | data formatting | bytes 40960000 | tf_op jit(solution)/shard_map/reshape | solution.py:273
  1452.1 17.2 %convert_reduce_fusion.6 = (f32[512]{0:T(512)S(1)}, bf16[1,512,1600]{1,2,0:T(8,128)(2,1)S(1)}) fusion(f32[1600]{0:T(1024)S(1)} %copy-done.39, bf16[1600,6400]{1,0:T(8,128)(2,1)} %reshape.642, bf16[1,512,1600]{1,2,0:T(8,128)(2,1)S(1)} %copy-done.19, bf16[512,6400]{1,0:T(8,128)(2,1)} %fusion.35.clone.1.clone.2), kind=kOutput, calls=%fused_computation.115 | convolution fusion | flops 10490675200 | bytes 30318848 | tf_op jit(solution)/shard_map/btf,fd->btd/dot_general | solution.py:240
  (192 shorter events, 423.0 us)
Async XLA Ops:
  670.2 18.4 %copy-start.27 = (f32[3,1600]{1,0:T(4,128)S(1)}, f32[3,1600]{1,0:T(4,128)}, u32[]{:S(2)}) copy-start(f32[3,1600]{1,0:T(4,128)} %param.21) | copy-start | bytes 57604
  670.2 18.4 %copy-start.28 = (f32[3,1600]{1,0:T(4,128)S(1)}, f32[3,1600]{1,0:T(4,128)}, u32[]{:S(2)}) copy-start(f32[3,1600]{1,0:T(4,128)} %param.20) | copy-start | bytes 57604
  670.2 19.1 %copy-start.10 = (bf16[1,512,1600]{1,2,0:T(8,128)(2,1)S(1)}, bf16[1,512,1600]{1,2,0:T(8,128)(2,1)}, u32[]{:S(2)}) copy-start(bf16[1,512,1600]{1,2,0:T(8,128)(2,1)} %param.17) | copy-start | bytes 4915204
  705.2 33.5 %copy-start.7 = (pred[512,512]{0,1:T(8,128)(4,1)}, pred[512,512]{0,1:T(8,128)(4,1)S(1)}, u32[]{:S(2)}) copy-start(pred[512,512]{0,1:T(8,128)(4,1)S(1)} %iota_compare_fusion) | copy-start | bytes 786436
  800.6 18.5 %copy-start.29 = (f32[3,1600]{1,0:T(4,128)S(1)}, f32[3,1600]{1,0:T(4,128)}, u32[]{:S(2)}) copy-start(f32[3,1600]{1,0:T(4,128)} %param.31) | copy-start | bytes 57604
  800.6 18.5 %copy-start.30 = (f32[3,1600]{1,0:T(4,128)S(1)}, f32[3,1600]{1,0:T(4,128)}, u32[]{:S(2)}) copy-start(f32[3,1600]{1,0:T(4,128)} %param.27) | copy-start | bytes 57604
  800.6 19.2 %copy-start.24 = (f32[3,6400]{1,0:T(4,128)S(1)}, f32[3,6400]{1,0:T(4,128)}, u32[]{:S(2)}) copy-start(f32[3,6400]{1,0:T(4,128)} %param.29) | copy-start | bytes 230404
  800.6 20.0 %copy-start.32 = (f32[3,1600]{1,0:T(4,128)S(1)}, f32[3,1600]{1,0:T(4,128)}, u32[]{:S(2)}) copy-start(f32[3,1600]{1,0:T(4,128)} %param.26) | copy-start | bytes 57604
  800.6 20.6 %copy-start.18 = (bf16[1,512,1600]{1,2,0:T(8,128)(2,1)S(1)}, bf16[1,512,1600]{1,2,0:T(8,128)(2,1)}, u32[]{:S(2)}) copy-start(bf16[1,512,1600]{1,2,0:T(8,128)(2,1)} %get-tuple-element.60) | copy-start | bytes 4915204
  821.2 22.8 %copy-start.16 = (bf16[4,4,2,2,6400]{4,3,1,0,2:T(2,128)(2,1)S(1)}, bf16[4,4,2,2,6400]{4,3,1,0,2:T(2,128)(2,1)}, u32[]{:S(2)}) copy-start(bf16[4,4,2,2,6400]{4,3,1,0,2:T(2,128)(2,1)} %get-tuple-element.42) | copy-start | bytes 2457604
  821.2 22.8 %copy-start.17 = (bf16[4,4,2,2,6400]{4,3,1,0,2:T(2,128)(2,1)S(1)}, bf16[4,4,2,2,6400]{4,3,1,0,2:T(2,128)(2,1)}, u32[]{:S(2)}) copy-start(bf16[4,4,2,2,6400]{4,3,1,0,2:T(2,128)(2,1)} %get-tuple-element.43) | copy-start | bytes 2457604
  1096.7 18.4 %copy-start.20 = (bf16[1,512,1600]{1,2,0:T(8,128)(2,1)S(1)}, bf16[1,512,1600]{1,2,0:T(8,128)(2,1)}, u32[]{:S(2)}) copy-start(bf16[1,512,1600]{1,2,0:T(8,128)(2,1)} %get-tuple-element.68) | copy-start | bytes 4915204
  1096.7 18.4 %copy-start.26 = (f32[6400]{0:T(1024)S(1)}, f32[6400]{0:T(1024)}, u32[]{:S(2)}) copy-start(f32[6400]{0:T(1024)} %get-tuple-element.9) | copy-start | bytes 76804
  1096.7 18.4 %copy-start.38 = (f32[1600]{0:T(1024)S(1)}, f32[1600]{0:T(1024)}, u32[]{:S(2)}) copy-start(f32[1600]{0:T(1024)} %get-tuple-element.12) | copy-start | bytes 19204
  1096.7 18.4 %copy-start.46 = (f32[1600]{0:T(1024)S(1)}, f32[1600]{0:T(1024)}, u32[]{:S(2)}) copy-start(f32[1600]{0:T(1024)} %get-tuple-element.90) | copy-start | bytes 19204
  1234.1 18.4 %copy-start.41 = (f32[1600]{0:T(1024)S(1)}, f32[1600]{0:T(1024)}, u32[]{:S(2)}) copy-start(f32[1600]{0:T(1024)} %get-tuple-element.25) | copy-start | bytes 19204
  1234.1 18.4 %copy-start.42 = (f32[1600]{0:T(1024)S(1)}, f32[1600]{0:T(1024)}, u32[]{:S(2)}) copy-start(f32[1600]{0:T(1024)} %get-tuple-element.89) | copy-start | bytes 19204
  1234.1 39.6 %slice-start.2 = ((s8[4915200]{0:T(1024)(128)(4,1)}), s8[720896]{0:T(1024)(128)(4,1)S(1)}, s32[]{:S(2)}) async-start(s8[4915200]{0:T(1024)(128)(4,1)} %bitcast.282), calls=%async_computation.2 | async-start | bytes 1441792
  1252.5 21.3 %slice-start.3 = ((s8[4915200]{0:T(1024)(128)(4,1)}), s8[4194304]{0:T(1024)(128)(4,1)S(1)}, s32[]{:S(2)}) async-start(s8[4915200]{0:T(1024)(128)(4,1)} %bitcast.282), calls=%async_computation.3 | async-start | bytes 8388608
  1375.0 18.4 %copy-start.19 = (bf16[1,512,1600]{1,2,0:T(8,128)(2,1)S(1)}, bf16[1,512,1600]{1,2,0:T(8,128)(2,1)}, u32[]{:S(2)}) copy-start(bf16[1,512,1600]{1,2,0:T(8,128)(2,1)} %get-tuple-element.76) | copy-start | bytes 4915204
  1375.1 18.4 %copy-start.25 = (f32[6400]{0:T(1024)S(1)}, f32[6400]{0:T(1024)}, u32[]{:S(2)}) copy-start(f32[6400]{0:T(1024)} %get-tuple-element.7) | copy-start | bytes 76804
  1375.1 18.4 %copy-start.36 = (f32[1600]{0:T(1024)S(1)}, f32[1600]{0:T(1024)}, u32[]{:S(2)}) copy-start(f32[1600]{0:T(1024)} %get-tuple-element.10) | copy-start | bytes 19204
  1375.1 18.4 %copy-start.40 = (f32[1600]{0:T(1024)S(1)}, f32[1600]{0:T(1024)}, u32[]{:S(2)}) copy-start(f32[1600]{0:T(1024)} %get-tuple-element.92) | copy-start | bytes 19204
  1393.5 22.5 %copy-start.11 = (bf16[4,4,2,2,6400]{4,3,1,0,2:T(2,128)(2,1)S(1)}, bf16[4,4,2,2,6400]{4,3,1,0,2:T(2,128)(2,1)}, u32[]{:S(2)}) copy-start(bf16[4,4,2,2,6400]{4,3,1,0,2:T(2,128)(2,1)} %get-tuple-element.38) | copy-start | bytes 2457604
  (27 other events, 344.1 us)

commit v2 on v1

v2 whole, which is shorter than its diff:
```python
import functools
import math

import jax
import jax.numpy as jnp
from jax import lax
from jax.experimental import pallas as pl
from jax.experimental.pallas import tpu as pltpu
from jax.sharding import PartitionSpec as P

MESH = pl.DeviceIdType.MESH
LANES = 128


class Torus:
    def __init__(self, axis, side, send_sem, recv_sem, local_sem):
        me = lax.axis_index(axis)
        self.axis, self.side = axis, side
        self.core = lax.rem(me, 2)
        self.x = lax.rem(me // 2, side)
        self.y = me // (2 * side)
        self.send_sem, self.recv_sem, self.local_sem = send_sem, recv_sem, local_sem

    def coord(self, dim, k):
        return lax.rem((self.x if dim == "x" else self.y) + (k + self.side), self.side)

    def device(self, y, x, core):
        return {self.axis: (y * self.side + x) * 2 + core}

    def step(self, dim, k):
        if dim == "x":
            return self.device(self.y, self.coord("x", k), self.core)
        return self.device(self.coord("y", k), self.x, self.core)

    def partner(self):
        return self.device(self.y, self.x, 1 - self.core)

    def meet(self):
        barrier = pltpu.get_barrier_semaphore()
        peers = [self.step(dim, k) for dim in ("x", "y") for k in (1, -1)] + [self.partner()]
        for peer in peers:
            pl.semaphore_signal(barrier, inc=1, device_id=peer, device_id_type=MESH)
        pl.semaphore_wait(barrier, len(peers))


class Unit:
    def __init__(self, torus, index, shard, landing):
        self.torus, self.index, self.shard, self.landing = torus, index, shard, landing
        half = shard.shape[-1] // LANES // 2 * LANES
        self.columns = (pl.ds(0, half), pl.ds(half, shard.shape[-1] - half))
        self.rank = len(shard.shape)
        cut = shard.shape[0] // 2
        self.rows = (slice(None), pl.ds(0, cut), pl.ds(cut, shard.shape[0] - cut))

    def _tail(self, t, part):
        return (self.rows[part],) + (slice(None),) * (self.rank - 2) + (self.columns[t],)

    def own(self, t):
        return self.shard.at[self._tail(t, 0)]

    def piece(self, t, k, part=0):
        torus = self.torus
        where = (torus.y, torus.coord("x", k)) if t == 0 else (torus.coord("y", k), torus.x)
        return self.landing.at[(torus.core,) + where + self._tail(t, part)]

    def block(self, t, k, part=0):
        torus = self.torus
        where = (torus.coord("y", k), slice(None)) if t == 0 else (slice(None), torus.coord("x", k))
        return self.landing.at[(torus.core,) + where + self._tail(t, part)]

    def copy(self, t, slot):
        torus = self.torus
        first, second = ("x", "y") if t == 0 else ("y", "x")
        source, target, device = {
            0: lambda: (self.own(t), self.piece(t, 0), torus.step(first, 1)),
            1: lambda: (self.own(t), self.piece(t, 0), torus.step(first, -1)),
            2: lambda: (self.piece(t, -1, 1), None, torus.step(first, 1)),
            3: lambda: (self.piece(t, 1, 2), None, torus.step(first, -1)),
            4: lambda: (self.block(t, 0), None, torus.step(second, 1)),
            5: lambda: (self.block(t, 0), None, torus.step(second, -1)),
            6: lambda: (self.block(t, -1, 1), None, torus.step(second, 1)),
            7: lambda: (self.block(t, 1, 2), None, torus.step(second, -1)),
            8: lambda: (self.block(t, 0), None, torus.partner()),
            9: lambda: (self.block(t, -1), None, torus.partner()),
            10: lambda: (self.block(t, 1), None, torus.partner()),
            11: lambda: (self.block(t, 2), None, torus.partner()),
        }[slot]()
        return pltpu.make_async_remote_copy(
            src_ref=source, dst_ref=source if target is None else target,
            send_sem=torus.send_sem.at[self.index, t, slot], recv_sem=torus.recv_sem.at[self.index, t, slot],
            device_id=device, device_id_type=MESH)

    def keep(self, t):
        return pltpu.make_async_copy(self.own(t), self.piece(t, 0), self.torus.local_sem.at[self.index, t])

    def start(self, *slots):
        for t in range(2):
            for slot in slots:
                self.copy(t, slot).start()

    def arrived(self, *slots):
        for t in range(2):
            for slot in slots:
                self.copy(t, slot).wait_recv()

    def send_own(self):
        self.start(0, 1)
        for t in range(2):
            self.keep(t).start()

    def relay_own(self):
        self.arrived(0, 1)
        self.start(2, 3)

    def send_block(self):
        for t in range(2):
            self.keep(t).wait()
        self.arrived(2, 3)
        self.start(4, 5, 8)

    def relay_block(self):
        self.arrived(4, 5)
        self.start(6, 7, 9, 10)

    def last_block(self):
        self.arrived(6, 7)
        self.start(11)

    def complete(self):
        self.arrived(8, 9, 10, 11)

    def drain(self):
        for t in range(2):
            for slot in range(12):
                self.copy(t, slot).wait_send()

TILE = 1280
CHUNK = 256
F32 = jnp.float32
BF16 = jnp.bfloat16


def dot(a, b, dims=((1,), (0,))):
    return lax.dot_general(a, b, (dims, ((), ())), preferred_element_type=F32)


def normalized(block):
    wide = block.astype(F32)
    centered = wide - jnp.mean(wide, axis=0, keepdims=True)
    return centered * lax.rsqrt(jnp.mean(centered * centered, axis=0, keepdims=True) + 1e-5)


def prefill_kernel(axis, side, heads, head_dim, shard, extra, hidden, k_cache, v_cache, gains, qkv_bias, up_bias, sides,
                   out, k_out, v_out, landing, landing_extra,
                   h_t, a_ref, qkv_t, o_t, u_ref, w_rest, w_buf, raw, acc, kc, vc,
                   send_sem, recv_sem, local_sem, w_sem, raw_sem, cache_sem, kv_sem):
    torus = Torus(axis, side, send_sem, recv_sem, local_sem)
    torus.meet()
    count = shard.shape[0]
    layers = count // 3
    model, tokens = h_t.shape
    cores, _, _, even = shard_rows = landing.shape[1:5]
    main = math.prod(shard_rows)
    half_main = main // cores
    rest = model - main
    inner = heads * head_dim
    prefix = kc.shape[-1]
    wide = shard.shape[-1]
    remote_rest = Unit(torus, count, extra, landing_extra)

    def unit(u):
        return Unit(torus, u, shard.at[u], landing.at[u])

    def push(u):
        unit(u).relay_block()

        @pl.when(u + 1 < count)
        def _():
            unit(u + 1).send_block()

        @pl.when(u + 3 < count)
        def _():
            unit(u + 3).send_own()

    def finish(u):
        unit(u).last_block()

        @pl.when(u + 2 < count)
        def _():
            unit(u + 2).relay_own()

        unit(u).complete()

    remote_rest.send_own()
    unit(0).send_own()
    unit(1).send_own()
    remote_rest.relay_own()
    unit(0).relay_own()
    remote_rest.send_block()
    remote_rest.relay_block()
    unit(0).send_block()
    unit(2).send_own()

    h_t[...] = hidden[...]
    o_t[pl.ds(0, LANES // 2), :] = jnp.zeros((LANES // 2, tokens), BF16)

    remote_rest.last_block()
    unit(1).relay_own()
    remote_rest.complete()

    def rest_copy(u):
        return pltpu.make_async_copy(landing_extra.at[:, :, :, u], raw, raw_sem)

    def spread(u, carry):
        rest_copy(u).start()
        rest_copy(u).wait()
        for i in range(cores):
            for j in range(side):
                for k in range(side):
                    at = ((i * side + j) * side + k) * raw.shape[3]
                    w_rest[u, at:at + raw.shape[3], :] = raw[i, j, k]
        return carry

    lax.fori_loop(0, count, spread, 0)
    push(0)
    finish(0)

    def w_copy(u, start, slot, size=TILE):
        return pltpu.make_async_copy(landing.at[u, :, :, :, :, pl.ds(start, size)],
                                     w_buf.at[slot, :, :, :, :, pl.ds(0, size)], w_sem.at[slot])

    def tiles(u, start_of, number, work):
        w_copy(u, start_of(0), 0).start()

        def turn(i, carry):
            slot = lax.rem(i, 2)

            @pl.when(i + 1 < number)
            def _():
                w_copy(u, start_of(i + 1), 1 - slot).start()

            w_copy(u, start_of(i), slot).wait()
            work(slot, start_of(i))
            return carry

        lax.fori_loop(0, number, turn, 0)

    def norm_rows(which, layer):
        gain = gains[layer, 2 * which:2 * which + 1, :]
        shift = gains[layer, 2 * which + 1:2 * which + 2, :]

        def turn(i, carry):
            at = pl.ds(pl.multiple_of(i * LANES, LANES), LANES)
            rows = jnp.transpose(normalized(h_t[:, at]))
            a_ref[at, :] = (rows * gain + shift).astype(BF16)
            return carry

        lax.fori_loop(0, tokens // LANES, turn, 0)

    def by_columns(u, slot, start, store):
        def turn(i, carry):
            local = pl.multiple_of(i * CHUNK, CHUNK)
            at = pl.ds(pl.multiple_of(start + local, LANES), CHUNK)
            w = w_buf[slot, :, :, :, :, pl.ds(local, CHUNK)].reshape(main, CHUNK)
            store(at, dot(a_ref[:, :main], w) + dot(a_ref[:, main:], w_rest[u, :, at]))
            return carry

        lax.fori_loop(0, TILE // CHUNK, turn, 0)

    def column(lane):
        lanes = lax.broadcasted_iota(jnp.int32, sides.shape, 1)
        return jnp.sum(jnp.where(lanes == lane, sides[...], 0.0), axis=1, keepdims=True)

    def add_rows(at, value, bias):
        h_t[at, :] = (h_t[at, :].astype(F32) + (value + bias)).astype(BF16)

    out_start = (3 * inner) // LANES * LANES
    first = TILE
    second = wide - out_start - first

    def head(h, carry):
        def rows(base):
            return pl.ds(pl.multiple_of(base + h * head_dim, head_dim), head_dim)

        query = qkv_t[rows(0), :]
        keys = jnp.concatenate([kc[rows(0), :], qkv_t[rows(inner), :]], axis=1)
        values = jnp.concatenate([vc[rows(0), :], qkv_t[rows(2 * inner), :]], axis=1)
        for b in range(tokens // CHUNK):
            upto = prefix + (b + 1) * CHUNK
            scores = dot(keys[:, :upto], query[:, b * CHUNK:(b + 1) * CHUNK], ((0,), (0,))) * (head_dim ** -0.5)
            position = lax.broadcasted_iota(jnp.int32, (upto, CHUNK), 0) - (upto - CHUNK)
            token = lax.broadcasted_iota(jnp.int32, (upto, CHUNK), 1)
            scores = jnp.where(position <= token, scores, -1e30)
            weights = jnp.exp(scores - jnp.max(scores, axis=0, keepdims=True))
            probs = (weights * (1.0 / jnp.sum(weights, axis=0, keepdims=True))).astype(BF16)
            o_t[rows(LANES // 2), b * CHUNK:(b + 1) * CHUNK] = dot(values[:, :upto], probs).astype(BF16)
        return carry

    def layer_turn(layer, carry):
        u = 3 * layer
        cached = [pltpu.make_async_copy(src.at[layer], dst, cache_sem.at[i])
                  for i, (src, dst) in enumerate(((k_cache, kc), (v_cache, vc)))]
        for copy in cached:
            copy.start()
        norm_rows(0, layer)

        def store_qkv(at, value):
            qkv_t[at, :] = jnp.transpose((value + qkv_bias[layer, :, at]).astype(BF16))

        last = qkv_t.shape[0] - TILE
        tiles(u, lambda i: pl.multiple_of(jnp.minimum(i * TILE, last), LANES), pl.cdiv(qkv_t.shape[0], TILE),
              lambda slot, start: by_columns(u, slot, start, store_qkv))
        w_copy(u, out_start, 0).start()
        w_copy(u, out_start + first, 1, second).start()
        fresh = [pltpu.make_async_copy(qkv_t.at[pl.ds((i + 1) * inner, inner), :], dst.at[layer], kv_sem.at[i])
                 for i, dst in enumerate((k_out, v_out))]
        for copy in fresh:
            copy.start()
        for copy in cached:
            copy.wait()
        early = heads // 2
        lax.fori_loop(0, early, head, 0)
        push(u + 1)
        lax.fori_loop(early, heads, head, 0)
        w_copy(u, out_start, 0).wait()
        w_copy(u, out_start + first, 1, second).wait()
        bias = column(2 * layer)
        for i in range(cores):
            at = slice(i * half_main, (i + 1) * half_main)
            value = dot(w_buf[0, i].reshape(half_main, TILE), o_t[:first, :])
            value += dot(w_buf[1, i, :, :, :, :second].reshape(half_main, second), o_t[first:, :])
            add_rows(at, value, bias[at])
        add_rows(slice(main, model), dot(w_rest[u, :, out_start:], o_t[...]), bias[main:])
        norm_rows(1, layer)
        for copy in fresh:
            copy.wait()

        finish(u + 1)

        def store_up(at, value):
            u_ref[:, at] = jax.nn.gelu(value + up_bias[layer, :, at], approximate=True).astype(BF16)

        tiles(u + 1, lambda i: pl.multiple_of(i * TILE, LANES), wide // TILE,
              lambda slot, start: by_columns(u + 1, slot, start, store_up))

        push(u + 2)
        finish(u + 2)
        acc[...] = jnp.zeros_like(acc)

        def down(slot, start):
            at = pl.ds(start, TILE)
            part = u_ref[:, at]
            for i in range(cores):
                acc[i * half_main:(i + 1) * half_main, :] += dot(w_buf[slot, i].reshape(half_main, TILE), part, ((1,), (1,)))
            acc[main:, :] += dot(w_rest[u + 2, :, at], part, ((1,), (1,)))

        tiles(u + 2, lambda i: pl.multiple_of(i * TILE, LANES), wide // TILE, down)
        add_rows(slice(None), acc[...], column(2 * layer + 1))

        @pl.when(layer + 1 < layers)
        def _():
            push(u + 3)
            finish(u + 3)

        return carry

    lax.fori_loop(0, layers, layer_turn, 0)
    gain, shift = column(2 * layers), column(2 * layers + 1)
    for i in range(tokens // LANES):
        at = slice(i * LANES, (i + 1) * LANES)
        out[:, at] = (normalized(h_t[:, at]) * gain + shift).astype(BF16)

    remote_rest.drain()

    def drain(u, carry):
        unit(u).drain()
        return carry

    lax.fori_loop(0, count, drain, 0)


def solution(mesh):
    part_axis, group_axis = mesh.axis_names
    side = math.isqrt(mesh.shape[group_axis] // 2)
    seq_spec = P((part_axis, group_axis))
    cache_spec = P(None, (part_axis, group_axis))
    replicated = P()
    in_specs = (seq_spec, cache_spec, cache_spec, replicated, replicated, P(None, group_axis), replicated,
                P(None, None, None, group_axis), replicated, replicated, replicated, P(None, group_axis), replicated,
                P(None, None, group_axis), replicated, replicated, replicated)
    out_specs = (seq_spec, cache_spec, cache_spec)

    def local_program(hidden, k_cache, v_cache, attn_gain, attn_shift, qkv_weight, qkv_bias, out_weight, out_bias, mlp_gain, mlp_shift, up_weight, up_bias, down_weight, down_bias, final_gain, final_shift):
        layers, depth, wide = up_weight.shape
        heads, head_dim = out_weight.shape[1:3]
        inner = heads * head_dim
        tokens, model = hidden.shape[1:]
        prefix = k_cache.shape[2]
        even = depth // 16 * 16
        odd = depth - even
        main = even * 2 * side * side
        w_q = qkv_weight.reshape(layers, depth, 3 * inner)
        w_o = jnp.transpose(out_weight, (0, 3, 1, 2)).reshape(layers, depth, inner)
        w_d = jnp.swapaxes(down_weight, 1, 2)
        shards = jnp.stack([jnp.concatenate([w_q, w_o], axis=2), up_weight, w_d], axis=1)
        shards = shards.reshape(layers * 3, depth, wide)

        def ordered(v):
            v = jnp.moveaxis(v.reshape((side, side, 2, depth) + v.shape[1:]), 2, 0)
            return jnp.concatenate([v[:, :, :, :even].reshape((main,) + v.shape[4:]),
                                    v[:, :, :, even:].reshape((model - main,) + v.shape[4:])])

        def restored(v):
            a = v[:main].reshape((2, side, side, even) + v.shape[1:])
            b = v[main:].reshape((2, side, side, odd) + v.shape[1:])
            return jnp.moveaxis(jnp.concatenate([a, b], axis=3), 0, 2).reshape(v.shape)

        gains = ordered(jnp.transpose(jnp.stack([attn_gain, attn_shift, mlp_gain, mlp_shift]), (2, 1, 0)))
        gains = jnp.transpose(gains, (1, 2, 0))
        sides = [v for i in range(layers) for v in (out_bias[i], down_bias[i])] + [final_gain, final_shift]
        sides = ordered(jnp.stack(sides, axis=1))

        def features(cache):
            return jnp.transpose(cache[:, 0], (0, 2, 3, 1)).reshape(layers, inner, prefix)

        any_space = pl.BlockSpec(memory_space=pl.ANY)
        vmem = pl.BlockSpec(memory_space=pltpu.VMEM)
        qkv_rows = pl.cdiv(3 * inner, LANES) * LANES
        bias = jnp.pad(qkv_bias.reshape(layers, 1, 3 * inner), ((0, 0), (0, 0), (0, qkv_rows - 3 * inner)))
        count = 3 * layers
        new = jax.ShapeDtypeStruct((layers, inner, tokens), BF16)
        dma = pltpu.SemaphoreType.DMA
        out, k_new, v_new, _, _ = pl.pallas_call(
            functools.partial(prefill_kernel, group_axis, side, heads, head_dim),
            out_shape=(jax.ShapeDtypeStruct((model, tokens), BF16), new, new,
                       jax.ShapeDtypeStruct((count, 2, side, side, even, wide), BF16),
                       jax.ShapeDtypeStruct((2, side, side, count, odd, wide), BF16)),
            in_specs=[vmem, vmem, vmem, any_space, any_space, vmem, vmem, vmem, vmem],
            out_specs=(vmem, any_space, any_space, any_space, any_space),
            scratch_shapes=[
                pltpu.VMEM((model, tokens), BF16),
                pltpu.VMEM((tokens, model), BF16),
                pltpu.VMEM((qkv_rows, tokens), BF16),
                pltpu.VMEM((LANES // 2 + inner, tokens), BF16),
                pltpu.VMEM((tokens, wide), BF16),
                pltpu.VMEM((count, model - main, wide), BF16),
                pltpu.VMEM((2, 2, side, side, even, TILE), BF16),
                pltpu.VMEM((2, side, side, odd, wide), BF16),
                pltpu.VMEM((model, tokens), F32),
                pltpu.VMEM((inner, prefix), BF16),
                pltpu.VMEM((inner, prefix), BF16),
                dma((count + 1, 2, 12)), dma((count + 1, 2, 12)), dma((count + 1, 2)),
                dma((2,)), dma, dma((2,)), dma((2,)),
            ],
            compiler_params=pltpu.CompilerParams(collective_id=0, has_side_effects=True, vmem_limit_bytes=67043328),
        )(shards[:, :even], shards[:, even:], ordered(hidden[0].T), features(k_cache), features(v_cache), gains, bias,
          up_bias.reshape(layers, 1, wide), sides)

        def tokens_first(v):
            return jnp.transpose(v.reshape(layers, 1, heads, head_dim, tokens), (0, 1, 4, 2, 3))

        return restored(out).T[None], tokens_first(k_new), tokens_first(v_new)

    return jax.shard_map(local_program, mesh=mesh, in_specs=in_specs, out_specs=out_specs, check_vma=False)
```

time: 1490 us -> 574 us (0.39); the launches traced: 1470 us -> 573 us
  local copies, waits for them, and re-layouts: 492 us -> 39.4 us
  matrix products: 285 us -> 0 us
  other arithmetic: 208 us -> 5.08 us
  Pallas kernels: 485 us -> 528 us
    dot_general x18 -> x0, matrix products: 243 us -> none  [the longest x3 67.4 us: decoder_layer(): jnp.einsum('btd,df->btf', normed_mlp, w_up, preferred_element_type=jnp.fl...]
    transpose x8 -> x1, local copies, waits for them, and re-layouts: 173 us -> 0.02 us  [local_program(): jnp.transpose(jnp.stack([attn_gain, attn_shift, mlp_gain, mlp_shift]), (2...]
    reshape x9 -> x10, local copies, waits for them, and re-layouts: 165 us -> 7.41 us  [the longest x2 2.74 us: ordered(): v = jnp.moveaxis(v.reshape((side, side, 2, depth) + v.shape[1:]), 2, 0)]
    concatenate x9 -> x0, local copies, waits for them, and re-layouts: 133 us -> none  [whole(): return jnp.concatenate([a, b], axis=3).reshape(model, wide)]
    concatenate x5 -> x2, other arithmetic: 125 us -> 2.22 us  [ordered(): jnp.concatenate([v[:, :, :, :even].reshape((main,) + v.shape[4:]), v[:, :...]
    reduce_sum x14 -> x0, other arithmetic: 64.5 us -> none  [the longest x3 49.6 us: attention(): jnp.sum(self_exp, axis=-1, keepdims=True)]
    pallas_call x1, Pallas kernels: 485 us -> 528 us  [local_program(): pl.pallas_call(functools.partial(prefill_kernel, group_axis, side, heads,...]
    unnamed x3 -> x0, matrix products: 41.9 us -> none
where the time goes in v2:
time: 574 us; the launch traced here: 573 us
  Pallas kernels  528 us (92%)
  local copies, waits for them, and re-layouts  39.4 us (7%)
    pallas_call x1, Pallas kernels, local_program(): pl.pallas_call(functools.partial(prefill_kernel, group_axis, side, heads,...  528 us
    unnamed x22, local copies, waits for them, and re-layouts  13.4 us

profile of v2, /device:TPU:97, one launch (start us, length us, event | category | flops | bytes accessed | tf_op | source)
XLA Modules:
  0.0 573.0 jit_solution(8249848483312880090)
XLA Ops:
  0.6 0.8 stack.63
  1.4 0.8 stack.64
  2.2 0.9 slice_reduce_fusion.1
  3.5 0.9 slice_reduce_fusion
  4.8 1.0 reshape.94
  6.5 1.6 reshape.95.up_bias
  8.0 0.8 maximum_bitcast_fusion.1
  12.1 0.9 pad_maximum_fusion.3.sides
  13.3 0.9 reshape.84
  14.2 2.4 reshape.86
  17.1 1.3 pad_maximum_fusion.2.hidden
  18.4 1.2 copy-done
  19.6 2.5 copy.80
  22.1 4.4 reshape.83
  26.8 1.3 copy-done.1
  28.8 0.8 pad_maximum_fusion
  30.0 0.8 slice.65.extra
  30.8 2.8 slice.64.shard
  33.7 527.6 %shard_map.184 = (bf16[1600,512]{1,0:T(8,128)(2,1)}, bf16[3,1600,512]{2,1,0:T(8,128)(2,1)}, bf16[3,1600,512]{2,1,0:T(8,128)(2,1)}, bf16[9,2,4,4,48,6400]{5,4,3,2...) custom-call(bf16[9,48,6400]{2,1,0:T(8,128)(2,1)} %slice.64.shard, bf16[9,2,6400]{2,1,0:T(2,128)(2,1)} %slice.65.extra, ...), custom_call_target="tpu_custom_call" | custom-call | tf_op jit(solution)/shard_map/pallas_call | solution.py:433
  561.3 0.8 slice.63
  562.1 1.5 slice.62
  563.9 1.4 reshape.100
  565.3 5.4 copy.109
  570.7 2.3 copy.110
  (47 shorter events, 6.9 us)
Async XLA Ops:
  9.5 3.5 copy-start.3
  17.1 2.5 copy-start
  26.5 1.6 copy-start.1
  26.5 2.2 copy-start.2
  563.9 6.8 %slice-start = ((s8[4915200]{0:T(1024)(128)(4,1)}), s8[720896]{0:T(1024)(128)(4,1)S(1)}, s32[]{:S(2)}) async-start(s8[4915200]{0:T(1024)(128)(4,1)} %bitcast.64), calls=%async_computation | async-start | bytes 1441792
  565.3 5.4 slice-start.1

commit v3 on v2

v3 whole, which is shorter than its diff:
```python
import functools
import math

import jax
import jax.numpy as jnp
from jax import lax
from jax.experimental import pallas as pl
from jax.experimental.pallas import tpu as pltpu
from jax.sharding import PartitionSpec as P

MESH = pl.DeviceIdType.MESH
LANES = 128


class Torus:
    def __init__(self, axis, side, send_sem, recv_sem, local_sem):
        me = lax.axis_index(axis)
        self.axis, self.side = axis, side
        self.core = lax.rem(me, 2)
        self.x = lax.rem(me // 2, side)
        self.y = me // (2 * side)
        self.send_sem, self.recv_sem, self.local_sem = send_sem, recv_sem, local_sem

    def coord(self, dim, k):
        return lax.rem((self.x if dim == "x" else self.y) + (k + self.side), self.side)

    def device(self, y, x, core):
        return {self.axis: (y * self.side + x) * 2 + core}

    def step(self, dim, k):
        if dim == "x":
            return self.device(self.y, self.coord("x", k), self.core)
        return self.device(self.coord("y", k), self.x, self.core)

    def partner(self):
        return self.device(self.y, self.x, 1 - self.core)

    def meet(self):
        barrier = pltpu.get_barrier_semaphore()
        peers = [self.step(dim, k) for dim in ("x", "y") for k in (1, -1)] + [self.partner()]
        for peer in peers:
            pl.semaphore_signal(barrier, inc=1, device_id=peer, device_id_type=MESH)
        pl.semaphore_wait(barrier, len(peers))


class Unit:
    def __init__(self, torus, index, shard, landing, parts=None):
        self.torus, self.index, self.shard, self.landing = torus, index, shard, landing
        half = shard.shape[-1] // LANES // 2 * LANES
        self.columns = (pl.ds(0, half), pl.ds(half, shard.shape[-1] - half))
        self.rank = len(shard.shape)
        self.parts = parts or (shard.shape[0],)

    def rows(self, part, third):
        base = 0 if part is None else sum(self.parts[:part])
        size = self.shard.shape[0] if part is None else self.parts[part]
        cut = size // 2
        return (pl.ds(base, size), pl.ds(base, cut), pl.ds(base + cut, size - cut))[third]

    def tail(self, t, part, third):
        return (self.rows(part, third),) + (slice(None),) * (self.rank - 2) + (self.columns[t],)

    def own(self, t):
        return self.shard.at[self.tail(t, None, 0)]

    def piece(self, t, k, third=0):
        torus = self.torus
        where = (torus.y, torus.coord("x", k)) if t == 0 else (torus.coord("y", k), torus.x)
        return self.landing.at[(torus.core,) + where + self.tail(t, None, third)]

    def block(self, t, k, part, third=0):
        torus = self.torus
        where = (torus.coord("y", k), slice(None)) if t == 0 else (slice(None), torus.coord("x", k))
        return self.landing.at[(torus.core,) + where + self.tail(t, part, third)]

    def copy(self, t, slot, part=0):
        torus = self.torus
        first, second = ("x", "y") if t == 0 else ("y", "x")
        source, target, device = {
            0: lambda: (self.own(t), self.piece(t, 0), torus.step(first, 1)),
            1: lambda: (self.own(t), self.piece(t, 0), torus.step(first, -1)),
            2: lambda: (self.piece(t, -1, 1), None, torus.step(first, 1)),
            3: lambda: (self.piece(t, 1, 2), None, torus.step(first, -1)),
            4: lambda: (self.block(t, 0, part), None, torus.step(second, 1)),
            5: lambda: (self.block(t, 0, part), None, torus.step(second, -1)),
            6: lambda: (self.block(t, -1, part, 1), None, torus.step(second, 1)),
            7: lambda: (self.block(t, 1, part, 2), None, torus.step(second, -1)),
            8: lambda: (self.block(t, 0, part), None, torus.partner()),
            9: lambda: (self.block(t, -1, part), None, torus.partner()),
            10: lambda: (self.block(t, 1, part), None, torus.partner()),
            11: lambda: (self.block(t, 2, part), None, torus.partner()),
        }[slot]()
        at = (self.index, t, slot)
        return pltpu.make_async_remote_copy(
            src_ref=source, dst_ref=source if target is None else target,
            send_sem=torus.send_sem.at[at], recv_sem=torus.recv_sem.at[at],
            device_id=device, device_id_type=MESH)

    def keep(self, t):
        return pltpu.make_async_copy(self.own(t), self.piece(t, 0), self.torus.local_sem.at[self.index, t])

    def start(self, *slots, part=0):
        for t in range(2):
            for slot in slots:
                self.copy(t, slot, part).start()

    def arrived(self, *slots, part=0):
        for t in range(2):
            for slot in slots:
                self.copy(t, slot, part).wait_recv()

    def send_own(self):
        self.start(0, 1)
        for t in range(2):
            self.keep(t).start()

    def relay_own(self):
        for t in range(2):
            for slot in (0, 1):
                self.copy(t, slot).wait_recv()
                self.copy(t, slot + 2).start()

    def send_block(self, part=0):
        if part == 0:
            for t in range(2):
                self.keep(t).wait()
            self.arrived(2, 3)
        self.start(4, 5, 8, part=part)

    def send_blocks(self):
        for part in range(len(self.parts)):
            self.send_block(part)

    def relay_block(self, part=0):
        for t in range(2):
            for slot in (4, 5):
                self.copy(t, slot, part).wait_recv()
                self.copy(t, slot + 2, part).start()
                self.copy(t, slot + 5, part).start()

    def last_block(self, part=0):
        self.arrived(6, 7, part=part)
        self.start(11, part=part)

    def complete(self, part=0):
        self.arrived(8, 9, 10, 11, part=part)

    def drain(self):
        for t in range(2):
            for slot in range(4):
                self.copy(t, slot).wait_send()
            for part in range(len(self.parts)):
                for slot in range(4, 12):
                    self.copy(t, slot, part).wait_send()


TILE = 1280
CHUNK = 256
F32 = jnp.float32
BF16 = jnp.bfloat16


def dot(a, b, dims=((1,), (0,))):
    return lax.dot_general(a, b, (dims, ((), ())), preferred_element_type=F32)


def normalized(block):
    wide = block.astype(F32)
    centered = wide - jnp.mean(wide, axis=0, keepdims=True)
    return centered * lax.rsqrt(jnp.mean(centered * centered, axis=0, keepdims=True) + 1e-5)


def prefill_kernel(axis, side, heads, head_dim, w_qkv, w_out, w_up, w_down, odd_rows, hidden, k_cache, v_cache,
                   vectors, qkv_bias, up_bias, out, k_out, v_out, landing, landing_extra,
                   shard, extra, packed, h_t, a_ref, qkv_t, o_t, u_ref, w_rest, w_buf, raw, acc, kc, vc, sides,
                   send_sem, recv_sem, local_sem, w_sem, raw_sem, cache_sem, kv_sem, fill_sem, pack_sem):
    torus = Torus(axis, side, send_sem, recv_sem, local_sem)
    count = shard.shape[0]
    layers = count // 3
    model, tokens = h_t.shape
    cores, _, _, even = shard_rows = landing.shape[1:5]
    main = math.prod(shard_rows)
    half_main = main // cores
    rest = model - main
    inner = heads * head_dim
    prefix = kc.shape[-1]
    wide = shard.shape[-1]
    remote_rest = Unit(torus, count, extra, landing_extra)

    def unit(layer, j):
        u = 3 * layer + j
        return Unit(torus, u, shard.at[u], landing.at[u])

    def exists(layer, j, work):
        if j < 3:
            work()
        else:
            pl.when(3 * layer + j < count)(work)

    def push(layer, j, part=0):
        unit(layer, j).relay_block(part)
        if part + 1 == len(unit(layer, j).parts):
            exists(layer, j + 3, lambda: unit(layer, j + 3).send_own())
            exists(layer, j + 1, lambda: unit(layer, j + 1).send_blocks())

    def finish(layer, j, part=0):
        unit(layer, j).last_block(part)
        if part == 0:
            exists(layer, j + 2, lambda: unit(layer, j + 2).relay_own())
        unit(layer, j).complete(part)

    fills = [pltpu.make_async_copy(src.at[i, pl.ds(0, even), :], shard.at[3 * i + k], fill_sem.at[2 * i + k - 1])
             for i in range(layers) for k, src in ((1, w_up), (2, w_down))]
    for copy in fills:
        copy.start()

    def pack(layer):
        blocks = 3 * heads
        sources = [pltpu.make_async_copy(w_qkv.at[layer], packed.at[pl.ds(0, blocks)], pack_sem.at[0]),
                   pltpu.make_async_copy(w_out.at[layer], packed.at[pl.ds(blocks, heads)], pack_sem.at[1])]
        for copy in sources:
            copy.start()
        for copy in sources:
            copy.wait()

        def turn(i, carry):
            at = pl.ds(pl.multiple_of(i * LANES, LANES), LANES)
            tile = jnp.concatenate([packed[2 * i], packed[2 * i + 1]], axis=1)
            shard[3 * layer, :, at] = tile[:even]
            extra[3 * layer, :, at] = tile[even:]
            return carry

        lax.fori_loop(0, wide // LANES, turn, 0)
        for k in (1, 2):
            extra[3 * layer + k] = odd_rows[2 * layer + k - 1]

    pack(0)
    torus.meet()
    unit(0, 0).send_own()
    for i in range(1, layers):
        pack(i)
    for copy in fills:
        copy.wait()
    remote_rest.send_own()
    unit(0, 1).send_own()
    unit(0, 0).relay_own()
    remote_rest.relay_own()
    unit(0, 0).send_blocks()
    unit(0, 1).relay_own()
    remote_rest.send_blocks()
    unit(0, 2).send_own()
    h_t[...] = hidden[...]
    o_t[pl.ds(0, LANES // 2), :] = jnp.zeros((LANES // 2, tokens), BF16)
    sides[...] = jnp.transpose(vectors[...])
    remote_rest.relay_block()
    push(0, 0)
    remote_rest.last_block()
    unit(0, 2).relay_own()
    remote_rest.complete()

    def rest_copy(u):
        return pltpu.make_async_copy(landing_extra.at[:, :, :, u], raw, raw_sem)

    def spread(u, carry):
        rest_copy(u).start()
        rest_copy(u).wait()
        for i in range(cores):
            for j in range(side):
                for k in range(side):
                    at = ((i * side + j) * side + k) * raw.shape[3]
                    w_rest[u, at:at + raw.shape[3], :] = raw[i, j, k]
        return carry

    lax.fori_loop(0, count, spread, 0)
    unit(0, 0).last_block()
    unit(0, 0).complete()

    def w_copy(u, start, slot, size=TILE, rows=(0, even)):
        at = pl.ds(*rows)
        return pltpu.make_async_copy(landing.at[u, :, :, :, at, pl.ds(start, size)],
                                     w_buf.at[slot, :, :, :, at, pl.ds(0, size)], w_sem.at[slot])

    def tiles(u, start_of, number, work, rows=(0, even)):
        w_copy(u, start_of(0), 0, rows=rows).start()

        def turn(i, carry):
            slot = lax.rem(i, 2)

            @pl.when(i + 1 < number)
            def _():
                w_copy(u, start_of(i + 1), 1 - slot, rows=rows).start()

            w_copy(u, start_of(i), slot, rows=rows).wait()
            work(slot, start_of(i))
            return carry

        lax.fori_loop(0, number, turn, 0)

    def norm_rows(which, layer):
        gain = vectors[pl.ds(2 * which * layers + layer, 1), :]
        shift = vectors[pl.ds((2 * which + 1) * layers + layer, 1), :]

        def turn(i, carry):
            at = pl.ds(pl.multiple_of(i * LANES, LANES), LANES)
            rows = jnp.transpose(normalized(h_t[:, at]))
            a_ref[at, :] = (rows * gain + shift).astype(BF16)
            return carry

        lax.fori_loop(0, tokens // LANES, turn, 0)

    def by_columns(u, slot, start, store):
        def turn(i, carry):
            local = pl.multiple_of(i * CHUNK, CHUNK)
            at = pl.ds(pl.multiple_of(start + local, LANES), CHUNK)
            w = w_buf[slot, :, :, :, :, pl.ds(local, CHUNK)].reshape(main, CHUNK)
            store(at, dot(a_ref[:, :main], w) + dot(a_ref[:, main:], w_rest[u, :, at]))
            return carry

        lax.fori_loop(0, TILE // CHUNK, turn, 0)

    def column(lane):
        lanes = lax.broadcasted_iota(jnp.int32, sides.shape, 1)
        return jnp.sum(jnp.where(lanes == lane, sides[...], 0.0), axis=1, keepdims=True)

    def add_rows(at, value, bias):
        h_t[at, :] = (h_t[at, :].astype(F32) + (value + bias)).astype(BF16)

    out_start = (3 * inner) // LANES * LANES
    first = TILE
    second = wide - out_start - first

    def head(h, carry):
        def rows(base):
            return pl.ds(pl.multiple_of(base + h * head_dim, head_dim), head_dim)

        query = qkv_t[rows(0), :]
        keys = jnp.concatenate([kc[rows(0), :], qkv_t[rows(inner), :]], axis=1)
        values = jnp.concatenate([vc[rows(0), :], qkv_t[rows(2 * inner), :]], axis=1)
        position = lax.broadcasted_iota(jnp.int32, (CHUNK, CHUNK), 0)
        token = lax.broadcasted_iota(jnp.int32, (CHUNK, CHUNK), 1)
        for b in range(tokens // CHUNK):
            upto = prefix + (b + 1) * CHUNK
            scores = dot(keys[:, :upto], query[:, b * CHUNK:(b + 1) * CHUNK], ((0,), (0,))) * (head_dim ** -0.5)
            diagonal = jnp.where(position <= token, scores[upto - CHUNK:], -1e30)
            scores = jnp.concatenate([scores[:upto - CHUNK], diagonal], axis=0)
            weights = jnp.exp(scores - jnp.max(scores, axis=0, keepdims=True))
            probs = (weights * (1.0 / jnp.sum(weights, axis=0, keepdims=True))).astype(BF16)
            o_t[rows(LANES // 2), b * CHUNK:(b + 1) * CHUNK] = dot(values[:, :upto], probs).astype(BF16)
        return carry

    def two_heads(i, carry):
        head(2 * i, carry)
        head(2 * i + 1, carry)
        return carry

    def layer_turn(layer, carry):
        u = 3 * layer
        cached = [pltpu.make_async_copy(src.at[layer], dst, cache_sem.at[i])
                  for i, (src, dst) in enumerate(((k_cache, kc), (v_cache, vc)))]
        for copy in cached:
            copy.start()
        norm_rows(0, layer)

        def store_qkv(at, value):
            qkv_t[at, :] = jnp.transpose((value + qkv_bias[pl.ds(layer, 1), at]).astype(BF16))

        last = qkv_t.shape[0] - TILE
        tiles(u, lambda i: pl.multiple_of(jnp.minimum(i * TILE, last), LANES), pl.cdiv(qkv_t.shape[0], TILE),
              lambda slot, start: by_columns(u, slot, start, store_qkv))
        w_copy(u, out_start, 0).start()
        w_copy(u, out_start + first, 1, second).start()
        fresh = [pltpu.make_async_copy(qkv_t.at[pl.ds((i + 1) * inner, inner), :], dst.at[layer], kv_sem.at[i])
                 for i, dst in enumerate((k_out, v_out))]
        for copy in fresh:
            copy.start()
        for copy in cached:
            copy.wait()
        early = heads // 4
        lax.fori_loop(0, early, two_heads, 0)
        push(layer, 1)
        lax.fori_loop(early, heads // 2, two_heads, 0)
        for i in range(heads // 2 * 2, heads):
            head(i, 0)
        w_copy(u, out_start, 0).wait()
        w_copy(u, out_start + first, 1, second).wait()
        bias = column(4 * layers + layer)
        for i in range(cores):
            at = slice(i * half_main, (i + 1) * half_main)
            value = dot(w_buf[0, i].reshape(half_main, TILE), o_t[:first, :])
            value += dot(w_buf[1, i, :, :, :, :second].reshape(half_main, second), o_t[first:, :])
            add_rows(at, value, bias[at])
        add_rows(slice(main, model), dot(w_rest[u, :, out_start:], o_t[...]), bias[main:])
        norm_rows(1, layer)
        for copy in fresh:
            copy.wait()

        finish(layer, 1)

        def store_up(at, value):
            u_ref[:, at] = jax.nn.gelu(value + up_bias[pl.ds(layer, 1), at], approximate=True).astype(BF16)

        tiles(u + 1, lambda i: pl.multiple_of(i * TILE, LANES), wide // TILE,
              lambda slot, start: by_columns(u + 1, slot, start, store_up))

        push(layer, 2)
        bias = column(5 * layers + layer)
        acc[...] = jnp.zeros_like(acc)
        finish(layer, 2)

        def down(slot, start):
            at = pl.ds(start, TILE)
            value = u_ref[:, at]
            for i in range(cores):
                w = w_buf[slot, i].reshape(half_main, TILE)
                acc[i * half_main:(i + 1) * half_main, :] += dot(w, value, ((1,), (1,)))
            acc[main:, :] += dot(w_rest[u + 2, :, at], value, ((1,), (1,)))

        tiles(u + 2, lambda i: pl.multiple_of(i * TILE, LANES), wide // TILE, down)
        add_rows(slice(None), acc[...], bias)

        @pl.when(layer + 1 < layers)
        def _():
            push(layer, 3)
            finish(layer, 3)

        return carry

    lax.fori_loop(0, layers, layer_turn, 0)
    gain, shift = column(6 * layers), column(6 * layers + 1)
    odd = rest // (cores * side * side)
    for part in range(tokens // LANES):
        lanes = slice(part * LANES, (part + 1) * LANES)
        value = (normalized(h_t[:, lanes]) * gain + shift).astype(BF16)
        for i in range(cores):
            for j in range(side * side):
                block = i * side * side + j
                at = (j * cores + i) * (even + odd)
                out[at:at + even, lanes] = value[block * even:(block + 1) * even]
                out[at + even:at + even + odd, lanes] = value[main + block * odd:main + (block + 1) * odd]

    remote_rest.drain()

    def drain(layer, carry):
        for j in range(3):
            unit(layer, j).drain()
        return carry

    lax.fori_loop(0, layers, drain, 0)


def solution(mesh):
    part_axis, group_axis = mesh.axis_names
    side = math.isqrt(mesh.shape[group_axis] // 2)
    seq_spec = P((part_axis, group_axis))
    cache_spec = P(None, (part_axis, group_axis))
    replicated = P()
    in_specs = (seq_spec, cache_spec, cache_spec, replicated, replicated, P(None, group_axis), replicated,
                P(None, None, None, group_axis), replicated, replicated, replicated, P(None, group_axis), replicated,
                P(None, None, group_axis), replicated, replicated, replicated)
    out_specs = (seq_spec, cache_spec, cache_spec)

    def local_program(hidden, k_cache, v_cache, attn_gain, attn_shift, qkv_weight, qkv_bias, out_weight, out_bias, mlp_gain, mlp_shift, up_weight, up_bias, down_weight, down_bias, final_gain, final_shift):
        layers, depth, wide = up_weight.shape
        heads, head_dim = out_weight.shape[1:3]
        inner = heads * head_dim
        tokens, model = hidden.shape[1:]
        prefix = k_cache.shape[2]
        even = depth // 16 * 16
        odd = depth - even
        main = even * 2 * side * side
        w_q = jnp.transpose(qkv_weight, (0, 2, 3, 1, 4)).reshape(layers, 3 * heads, depth, head_dim)
        w_o = jnp.transpose(out_weight, (0, 1, 3, 2))
        w_d = jnp.swapaxes(down_weight, 1, 2)
        odd_rows = jnp.stack([up_weight[:, even:], w_d[:, even:]], axis=1).reshape(2 * layers, odd, wide)

        def ordered(v):
            v = jnp.moveaxis(v.reshape((side, side, 2, depth) + v.shape[1:]), 2, 0)
            return jnp.concatenate([v[:, :, :, :even].reshape((main,) + v.shape[4:]),
                                    v[:, :, :, even:].reshape((model - main,) + v.shape[4:])])

        rows = [attn_gain, attn_shift, mlp_gain, mlp_shift, out_bias, down_bias, final_gain[None], final_shift[None]]
        rows += [jnp.zeros((-(6 * layers + 2) % 8, model), F32)]
        vectors = jnp.concatenate(rows).reshape(-1, side * side, 2, depth).swapaxes(1, 2)
        vectors = jnp.concatenate([vectors[..., :even].reshape(-1, main), vectors[..., even:].reshape(-1, model - main)], axis=1)

        def features(cache):
            return jnp.transpose(cache[:, 0], (0, 2, 3, 1)).reshape(layers, inner, prefix)

        any_space = pl.BlockSpec(memory_space=pl.ANY)
        vmem = pl.BlockSpec(memory_space=pltpu.VMEM)
        qkv_rows = pl.cdiv(3 * inner, LANES) * LANES
        bias = jnp.pad(qkv_bias.reshape(layers, 3 * inner), ((0, 0), (0, qkv_rows - 3 * inner)))
        count = 3 * layers
        new = jax.ShapeDtypeStruct((layers, inner, tokens), BF16)
        dma = pltpu.SemaphoreType.DMA
        out, k_new, v_new, _, _ = pl.pallas_call(
            functools.partial(prefill_kernel, group_axis, side, heads, head_dim),
            out_shape=(jax.ShapeDtypeStruct((model, tokens), BF16), new, new,
                       jax.ShapeDtypeStruct((count, 2, side, side, even, wide), BF16),
                       jax.ShapeDtypeStruct((2, side, side, count, odd, wide), BF16)),
            in_specs=[any_space] * 4 + [vmem, vmem, any_space, any_space, vmem, vmem, vmem],
            out_specs=(vmem, any_space, any_space, any_space, any_space),
            scratch_shapes=[
                pltpu.VMEM((count, even, wide), BF16),
                pltpu.VMEM((count, odd, wide), BF16),
                pltpu.VMEM((4 * heads, depth, head_dim), BF16),
                pltpu.VMEM((model, tokens), BF16),
                pltpu.VMEM((tokens, model), BF16),
                pltpu.VMEM((qkv_rows, tokens), BF16),
                pltpu.VMEM((LANES // 2 + inner, tokens), BF16),
                pltpu.VMEM((tokens, wide), BF16),
                pltpu.VMEM((count, model - main, wide), BF16),
                pltpu.VMEM((2, 2, side, side, even, TILE), BF16),
                pltpu.VMEM((2, side, side, odd, wide), BF16),
                pltpu.VMEM((model, tokens), F32),
                pltpu.VMEM((inner, prefix), BF16),
                pltpu.VMEM((inner, prefix), BF16),
                pltpu.VMEM((model, vectors.shape[0]), F32),
                dma((count + 1, 2, 12)), dma((count + 1, 2, 12)), dma((count + 1, 2)),
                dma((2,)), dma, dma((2,)), dma((2,)), dma((2 * layers,)), dma((2,)),
            ],
            compiler_params=pltpu.CompilerParams(collective_id=0, has_side_effects=True, vmem_limit_bytes=67043328),
        )(w_q, w_o, up_weight, w_d, odd_rows, ordered(hidden[0].T), features(k_cache), features(v_cache), vectors, bias,
          up_bias)

        def tokens_first(v):
            return jnp.transpose(v.reshape(layers, 1, heads, head_dim, tokens), (0, 1, 4, 2, 3))

        return out.T[None], tokens_first(k_new), tokens_first(v_new)

    return jax.shard_map(local_program, mesh=mesh, in_specs=in_specs, out_specs=out_specs, check_vma=False)
```

time: 574 us -> 557 us (0.970)
  local copies, waits for them, and re-layouts: 39.4 us -> 22.7 us
    reshape x8 -> x3, local copies, waits for them, and re-layouts: 9.87 us -> 1.29 us  [the longest x1 1.02 us: local_program(): qkv_bias.reshape(layers, 3 * inner)]
    slice x6 -> x2, local copies, waits for them, and re-layouts: 7.82 us -> 0.47 us  [local_program(): vectors[..., even:].reshape(-1, model - main)]
    concatenate x0 -> x9, local copies, waits for them, and re-layouts: none -> 7.03 us  [local_program(): jnp.concatenate(rows).reshape(-1, side * side, 2, depth).swapaxes(1, 2)]
    unnamed x22 -> x17, local copies, waits for them, and re-layouts: 13.4 us -> 10.5 us
where the time goes in v3:
time: 557 us; the launch traced here: 556 us
  Pallas kernels  530 us (95%)
  local copies, waits for them, and re-layouts  22.7 us (4%)
    pallas_call x1, Pallas kernels, local_program(): pl.pallas_call(functools.partial(prefill_kernel, group_axis, side, heads,...  530 us

profile of v3, /device:TPU:97, one launch (start us, length us, event | category | flops | bytes accessed | tf_op | source)
XLA Modules:
  0.0 555.5 jit_solution(14744310245463335611)
XLA Ops:
  0.6 0.8 concatenate.33
  1.4 0.8 concatenate.34
  2.2 0.9 concatenate.27
  3.1 0.9 concatenate.28
  4.0 0.9 concatenate.31
  4.9 0.9 concatenate.29
  5.8 1.0 concatenate.30
  6.8 0.9 concatenate.32
  7.7 1.0 reshape.63
  8.7 0.7 pad.4.qkv_bias
  9.4 1.1 slice_bitcast_fusion
  10.5 0.2 pad_maximum_fusion.2
  10.7 0.8 copy.54
  11.6 0.2 reshape.61
  11.8 0.2 slice.28
  12.0 0.3 copy.65
  12.4 0.7 pad_maximum_fusion.1.vectors
  13.1 0.5 reshape.56
  13.6 0.2 slice.25
  14.0 1.3 pad_maximum_fusion.hidden
  15.2 529.8 %shard_map.184 = (bf16[1600,512]{1,0:T(8,128)(2,1)}, bf16[3,1600,512]{2,1,0:T(8,128)(2,1)}, bf16[3,1600,512]{2,1,0:T(8,128)(2,1)}, bf16[9,2,4,4,48,6400]{5,4,3,2...) custom-call(bf16[3,75,50,64]{3,2,1,0:T(8,128)(2,1)} %bitcast.50, bf16[3,25,50,64]{3,2,1,0:T(8,128)(2,1)} %bitcast.59, ...), custom_call_target="tpu_custom_call" | custom-call | tf_op jit(solution)/shard_map/pallas_call | solution.py:496
  545.1 2.9 copy.88
  548.0 5.3 copy.89
  553.3 2.3 copy.90
  (21 shorter events, 0.3 us)
Async XLA Ops:
  5.8 7.3 %copy-start = (bf16[1,512,1600]{1,2,0:T(8,128)(2,1)S(1)}, bf16[1,512,1600]{1,2,0:T(8,128)(2,1)}, u32[]{:S(2)}) copy-start(bf16[1,512,1600]{1,2,0:T(8,128)(2,1)} %param.17) | copy-start | bytes 4915204
  545.1 8.2 %slice-start = ((s8[4915200]{0:T(1024)(128)(4,1)}), s8[4194304]{0:T(1024)(128)(4,1)S(1)}, s32[]{:S(2)}) async-start(s8[4915200]{0:T(1024)(128)(4,1)} %bitcast.46), calls=%async_computation | async-start | bytes 8388608
  548.0 5.3 slice-start.1
